TPU v7x, 1024 devices: a whole 4x8x16 slice. The times are simulated.
1024 devices in a mesh: dom: 256 (over z, y, core), grp: 4 (over x).
Axes of the slice: x: 4, y: 8, z: 16, core: 2. Of those that a mesh axis runs over, the one named last changes fastest.
Arguments:
- positions: float32 [3, 1048576], P(None, ('dom', 'grp')), may hold values from 0 to 65, as said below
- velocity: float32 [3, 1048576], P(None, ('dom', 'grp')), may hold values from -6 to 6
- smoothing: float32 [1048576], P(('dom', 'grp')), may hold values from 0.24 to 0.4
- mass: float32 [1048576], P(('dom', 'grp')), may hold values from 0.002 to 0.02
- energy: float32 [1048576], P(('dom', 'grp')), may hold values from 0.5 to 4
- targets: int32 [8192, 1], P(('dom', 'grp')), may hold values from 0 to 3; in each aligned block of 8 rows (0 to 7, 8 to 15, ...) at most 4 rows name the same one
- neighbours: int32 [8192, 4], P(('dom', 'grp')), may hold values from 0 to 143
- counts: int32 [8192], P(('dom', 'grp')), may hold values from 1 to 128
Outputs:
- density: float32 [2097152], P(('dom', 'grp'))
- accel: float32 [3, 2097152], P(None, ('dom', 'grp'))
- timestep: float32 [1], replicated
Inputs may be any that keep to these rules, and one draw needn't show every extreme that they name: `targets`: each device sends at most 4 blocks to one index of grp, and exactly 4 in some draws' devices. `positions`: the particles of a block of a device with index a along dom have first component within a / 4 to a / 4 + 1, the others within 0 to 1.
All inputs are finite; a program needn't handle non-finite values.
Results may differ from a plain program's by a relative error of at most 0.0003.
Values sent between devices are 32-bit elements; how exact they have to be, the bound alone decides.
A program may use at most 32 MiB of HBM per device.

v0:
```python
import functools
import math

import jax
import jax.numpy as jnp
from jax import lax
from jax.sharding import Mesh
from jax.sharding import PartitionSpec as P

CAP = 4
DOM_GRP = ("dom_0", "dom_1", "dom_2", "grp")
DOM = ("dom_0", "dom_1", "dom_2")


DRIFT = 0.05
GAMMA = 5.0 / 3.0
CFL = 0.3
KNORM = 315.0 / (64.0 * math.pi)


def in_one_piece(arrays, axis, split_dim, concat_dim, along):
    widths = [math.prod(a.shape[along:]) for a in arrays]
    both = jnp.concatenate(
        [a.reshape(*a.shape[:along], w) for a, w in zip(arrays, widths)], axis=along
    )
    result = lax.all_to_all(both, axis, split_axis=split_dim, concat_axis=concat_dim, tiled=True)
    pieces = jnp.split(result, [sum(widths[:k]) for k in range(1, len(widths))], axis=along)
    return tuple(
        (b.reshape(*result.shape[:along], *a.shape[along:]) for a, b in zip(arrays, pieces))
    )


def padded(cells, sides, width):
    for axis, dim in sides:
        count = lax.axis_size(axis)
        ends = count - 1
        head = lax.slice_in_dim(cells, 0, width, axis=dim)
        tail = lax.slice_in_dim(cells, cells.shape[dim] - width, cells.shape[dim], axis=dim)
        cells = jnp.concatenate(
            [
                lax.ppermute(tail, axis, [(i, (i + 1) % count) for i in range(ends)]),
                cells,
                lax.ppermute(head, axis, [((i + 1) % count, i) for i in range(ends)]),
            ],
            axis=dim,
        )
    return cells


def over_axes(value, axes):
    return functools.reduce(lax.pmin, axes, value)


def partner_sums(own_x, own_h, part_x, part_m, part_f, own_f):
    dsq = jnp.zeros(part_m.shape[:2] + (own_x.shape[2], part_m.shape[2]), jnp.float32)
    diffs = []
    for comp in range(3):
        delta = own_x[:, None, comp, :, None] - part_x[:, :, comp, None, :]
        diffs.append(delta)
        dsq = dsq + delta * delta
    inv_h = 1.0 / own_h
    base = jnp.maximum(1.0 - dsq * (inv_h * inv_h)[:, None, :, None], 0.0)
    rho = KNORM * inv_h**3 * jnp.sum(part_m[:, :, None, :] * base**3, axis=(1, 3))
    if part_f is None:
        return rho
    coef = part_m[:, :, None, :] * (own_f[:, None, :, None] + part_f[:, :, None, :]) * base * base
    acc = jnp.stack([jnp.sum(coef * diffs[c], axis=(1, 3)) for c in range(3)], axis=1)
    return 6.0 * KNORM * (inv_h**5)[:, None, :] * acc


def body(positions, velocity, smoothing, mass, energy, targets, neighbours, counts):
    nblk = counts.shape[0]
    width = positions.shape[1] // nblk
    groups = lax.axis_size("grp")
    slots = groups * CAP
    drifted = positions + DRIFT * velocity
    fields = jnp.concatenate([drifted, smoothing[None], mass[None], energy[None]], axis=0)
    flat = fields.reshape(6, nblk, width).transpose(1, 0, 2).reshape(nblk, 6 * width)
    target = targets[:, 0]
    onehot = (target[:, None] == jnp.arange(groups, dtype=jnp.int32)[None, :]).astype(jnp.int32)
    rank = jnp.sum((jnp.cumsum(onehot, axis=0) - onehot) * onehot, axis=1)
    slot_of = target * CAP + rank
    picker = jnp.arange(slots, dtype=jnp.int32)[:, None] == slot_of[None, :]
    send_fields = jnp.dot(
        picker.astype(jnp.float32),
        flat,
        precision=lax.Precision.HIGHEST,
        preferred_element_type=jnp.float32,
    )
    picker_int = picker.astype(jnp.int32)
    send_nbr = jnp.dot(picker_int, neighbours, preferred_element_type=jnp.int32)
    send_cnt = jnp.dot(picker_int, counts[:, None], preferred_element_type=jnp.int32)[:, 0]
    got_fields, got_nbr, got_cnt = (
        lax.all_to_all(
            send_fields.reshape(groups, CAP, 6, width),
            "grp",
            split_axis=0,
            concat_axis=0,
            tiled=True,
        ),
        *in_one_piece(
            (send_nbr.reshape(groups, CAP, -1), send_cnt.reshape(groups, CAP)), "grp", 0, 0, 2
        ),
    )
    slot_fields = got_fields.reshape(slots, 6, width)
    slot_nbr = got_nbr.reshape(slots, -1)
    slot_cnt = got_cnt.reshape(slots)
    live = slot_cnt > 0
    hval = jnp.where(live[:, None], slot_fields[:, 3], 1.0)
    own_xm = jnp.concatenate([slot_fields[:, 0:3], slot_fields[:, 4:5]], axis=1)
    ghost_pool = padded(own_xm[None, None], ((DOM, 0), ("grp", 1)), 1)
    ghost_pool = ghost_pool.reshape(9 * slots, 4, width)
    own_index = 4 * slots + jnp.arange(slots, dtype=jnp.int32)
    partner_idx = jnp.concatenate([own_index[:, None], slot_nbr], axis=1)
    chosen = ghost_pool[partner_idx]
    rho = partner_sums(slot_fields[:, 0:3], hval, chosen[:, :, 0:3], chosen[:, :, 3], None, None)
    rho_safe = jnp.where(live[:, None], rho, 1.0)
    factor = jnp.where(live[:, None], (GAMMA - 1.0) * slot_fields[:, 5] / rho_safe, 0.0)
    packed = jnp.concatenate([own_xm, factor[:, None]], axis=1)
    second = padded(packed[None, None], ((DOM, 0), ("grp", 1)), 1)
    second = second.reshape(9 * slots, 5, width)[partner_idx]
    part_x, part_m, part_f = (second[:, :, 0:3], second[:, :, 3], second[:, :, 4])
    acc = partner_sums(slot_fields[:, 0:3], hval, part_x, part_m, part_f, factor)
    active = jnp.arange(width, dtype=jnp.int32)[None, :] < slot_cnt[:, None]
    acc = jnp.where(active[:, None, :], acc, 0.0)
    density = jnp.where(live[:, None], rho, 0.0).reshape(-1)
    accel = acc.transpose(1, 0, 2).reshape(3, -1)
    sound = jnp.sqrt(GAMMA * (GAMMA - 1.0) * jnp.where(active, slot_fields[:, 5], 1.0))
    local_least = jnp.min(jnp.where(active, CFL * hval / sound, 1e30))
    timestep = over_axes(local_least, DOM_GRP).reshape(1)
    return (density, accel, timestep)


def solution(mesh):
    torus = Mesh(
        mesh.devices.reshape(16, 8, 2, mesh.shape["grp"]), ("dom_0", "dom_1", "dom_2", "grp")
    )
    placed = (
        P(None, DOM_GRP),
        P(None, DOM_GRP),
        P(DOM_GRP),
        P(DOM_GRP),
        P(DOM_GRP),
        P(DOM_GRP, None),
        P(DOM_GRP, None),
        P(DOM_GRP),
    )
    return jax.shard_map(
        body,
        mesh=torus,
        in_specs=placed,
        out_specs=(P(DOM_GRP), P(None, DOM_GRP), P()),
        check_vma=False,
    )
```

profile of v0, /device:TPU:68, one launch (start us, length us, event | category | flops | bytes accessed | tf_op | source)
XLA Modules:
  0.0 136.3 jit_solution(10335752635936781529)
XLA Ops:
  0.6 0.0 copy-start
  0.7 0.7 fusion.46
  1.3 0.2 reduce_window_sum.11
  1.5 0.7 select_reduce_fusion
  2.2 0.7 multiply_add_fusion.1
  2.8 0.0 copy-done
  2.8 0.1 fusion.39
  3.0 0.1 reshape.298
  3.1 1.0 fusion.20
  4.1 0.7 copy.80
  4.8 4.8 %all-to-all-start = ((s32[4,4,5]{2,1,0:T(4,128)}), s32[4,4,5]{2,1,0:T(4,128)S(1)}, u32[]{:S(2)}, u32[]{:S(2)}) async-start(s32[4,4,5]{2,1,0:T(4,128)} %copy.80), calls=%async_computation | async-start | bytes 16384 | tf_op jit(solution)/shard_map/all_to_all | solution.py:26
  9.6 0.7 add_bitcast_fusion
  10.3 1.6 %fusion.10 = f32[4,4,6,128]{3,1,2,0:T(4,128)} fusion(f32[1,8,128]{2,1,0:T(8,128)} %bitcast.164, f32[1,8,128]{2,1,0:T(8,128)} %bitcast.165, f32[1,8,128]{2,1,0:T(8,128)} %bitcast.166, f32[3,8,128]{2,1,0:T(8,128)S(1)} %bitcast.159, s32[8]{0:T(128)S(1)} %multiply_add_fusion.1, s32[4,4]{1,0:T(4,128)S(1)} %multiply_add_fusion), kind=kOutput, calls=%fused_computation.37 | convolution fusion | flops 1198208 | bytes 73824 | tf_op jit(solution)/shard_map/dot_general | solution.py:84
  11.9 0.6 all-to-all-done
  12.5 5.6 %all-to-all-start.1 = ((f32[4,4,6,128]{3,1,2,0:T(4,128)}), f32[4,4,6,128]{3,1,2,0:T(4,128)S(1)}, u32[]{:S(2)}, u32[]{:S(2)}) async-start(f32[4,4,6,128]{3,1,2,0:T(4,128)} %fusion.10), calls=%async_computation.1 | async-start | bytes 98304 | tf_op jit(solution)/shard_map/all_to_all | solution.py:94
  18.1 0.2 slice_reduce_fusion
  18.3 0.1 reshape_reshape.3
  18.4 0.1 iota_compare_fusion
  18.5 0.1 copy.100
  18.6 0.1 copy.85
  18.7 2.5 %all-to-all-done.1 = f32[4,4,6,128]{3,1,2,0:T(4,128)S(1)} async-done(((f32[4,4,6,128]{3,1,2,0:T(4,128)}), f32[4,4,6,128]{3,1,2,0:T(4,128)S(1)}, u32[]{:S(2)}, u32[]{:S(2)}) %all-to-all-start.1) | async-done | bytes 49184 | tf_op jit(solution)/shard_map/all_to_all | solution.py:94
  21.2 1.9 %collective-permute-start.1 = (f32[1,1,16,4,128]{4,2,3,1,0:T(8,128)S(1)}, f32[1,1,16,4,128]{4,2,3,1,0:T(8,128)S(1)}, u32[]{:S(2)}, u32[]{:S(2)}) collective-permute-start(f32[1,1,16,4,128]{4,2,3,1,0:T(8,128)S(1)} %maximum_bitcast_fusion.1), channel_id=1, source_target_pairs={{4,0},{8,4},{12,8},{16,12},{20,16},{24,20},{28,24},{32,28},{36,32}... | collective-permute-start | bytes 98312 | tf_op jit(solution)/shard_map/ppermute | solution.py:43
  23.2 2.4 %collective-permute-start = (f32[1,1,16,4,128]{4,2,3,1,0:T(8,128)S(1)}, f32[1,1,16,4,128]{4,2,3,1,0:T(8,128)S(1)}, u32[]{:S(2)}, u32[]{:S(2)}) collective-permute-start(f32[1,1,16,4,128]{4,2,3,1,0:T(8,128)S(1)} %maximum_bitcast_fusion.1), channel_id=1, source_target_pairs={{0,4},{4,8},{8,12},{12,16},{16,20},{20,24},{24,28},{28,32},{32,36}... | collective-permute-start | bytes 98312 | tf_op jit(solution)/shard_map/ppermute | solution.py:41
  25.6 0.7 fusion.38
  26.2 40.9 %pmin.28 = f32[]{:T(128)} all-reduce(f32[]{:T(128)} %get-tuple-element.15), channel_id=1, replica_groups=mesh['dom_0'=16,'dom_1'=8,'dom_2'=2,'grp'=4] {'dom_0'}, use_global_device_ids=true, to_apply=%region_7.8 | all-reduce | flops 1 | bytes 8 | tf_op jit(solution)/shard_map/pmin | solution.py:51
  67.2 0.1 reshape.307
  67.2 18.3 %pmin.29 = f32[]{:T(128)} all-reduce(f32[]{:T(128)} %pmin.28), channel_id=1, replica_groups=mesh['dom_0'=16,'dom_1'=8,'dom_2'=2,'grp'=4] {'dom_1'}, use_global_device_ids=true, to_apply=%region_8.9 | all-reduce | flops 1 | bytes 8 | tf_op jit(solution)/shard_map/pmin | solution.py:51
  85.5 0.0 collective-permute-done.1
  85.5 0.0 collective-permute-done
  85.5 3.5 %collective-permute-start.3 = (f32[3,1,16,4,128]{4,2,3,1,0:T(8,128)S(1)}, f32[3,1,16,4,128]{4,2,3,1,0:T(8,128)S(1)}, u32[]{:S(2)}, u32[]{:S(2)}) collective-permute-start(f32[3,1,16,4,128]{4,2,3,1,0:T(8,128)S(1)} %pad_maximum_fusion.3), channel_id=1, source_target_pairs={{1,0},{2,1},{3,2},{5,4},{6,5},{7,6},{9,8},{10,9},{11,10},{13,12},{... | collective-permute-start | bytes 294920 | tf_op jit(solution)/shard_map/ppermute | solution.py:43
  89.0 2.3 %collective-permute-start.2 = (f32[3,1,16,4,128]{4,2,3,1,0:T(8,128)S(1)}, f32[3,1,16,4,128]{4,2,3,1,0:T(8,128)S(1)}, u32[]{:S(2)}, u32[]{:S(2)}) collective-permute-start(f32[3,1,16,4,128]{4,2,3,1,0:T(8,128)S(1)} %pad_maximum_fusion.3), channel_id=1, source_target_pairs={{0,1},{1,2},{2,3},{4,5},{5,6},{6,7},{8,9},{9,10},{10,11},{12,13},{... | collective-permute-start | bytes 294920 | tf_op jit(solution)/shard_map/ppermute | solution.py:41
  91.4 3.1 %pmin.30 = f32[]{:T(128)} all-reduce(f32[]{:T(128)} %pmin.29), channel_id=1, replica_groups=mesh['dom_0'=16,'dom_1'=8,'dom_2'=2,'grp'=4] {'dom_2'}, use_global_device_ids=true, to_apply=%region_9.10 | all-reduce | flops 1 | bytes 8 | tf_op jit(solution)/shard_map/pmin | solution.py:51
  94.5 8.7 %pmin.31 = f32[1]{0:T(128)} all-reduce(f32[1]{0:T(128)} %bitcast.52), channel_id=1, replica_groups=mesh['dom_0'=16,'dom_1'=8,'dom_2'=2,'grp'=4] {'grp'}, use_global_device_ids=true, to_apply=%region_10.11 | all-reduce | flops 1 | bytes 8 | tf_op jit(solution)/shard_map/pmin | solution.py:51
  103.2 0.0 collective-permute-done.3
  103.2 0.0 collective-permute-done.2
  103.3 0.1 copy.86
  103.4 0.7 gather_fusion
  104.1 0.1 fusion.51
  104.3 3.4 %fusion.9 = f32[16,128]{1,0:T(8,128)S(1)} fusion(f32[16,128]{1,0:T(8,128)S(1)} %get-tuple-element.16, f32[16,5,128]{2,1,0:T(8,128)S(1)} %get-tuple-element.23, f32[16,128]{1,0:T(8,128)S(1)} %get-tuple-element.20, f32[16,5,128]{2,1,0:T(8,128)S(1)} %get-tuple-element.24, f32[16,128]{1,0:T(8,128)S(1)} %get-tuple-element.21, ...), kind=kLoop, calls=%fused_computation.19 | loop fusion | flops 19658752 | bytes 204800 | tf_op jit(solution)/shard_map/reduce_sum | solution.py:63
  107.7 0.1 fusion.23
  107.8 2.7 %collective-permute-start.5 = (f32[1,1,16,5,128]{4,2,3,1,0:T(8,128)S(1)}, f32[1,1,16,5,128]{4,2,3,1,0:T(8,128)S(1)}, u32[]{:S(2)}, u32[]{:S(2)}) collective-permute-start(f32[1,1,16,5,128]{4,2,3,1,0:T(8,128)S(1)} %maximum_bitcast_fusion), channel_id=1, source_target_pairs={{4,0},{8,4},{12,8},{16,12},{20,16},{24,20},{28,24},{32,28},{36,32}... | collective-permute-start | bytes 122888 | tf_op jit(solution)/shard_map/ppermute | solution.py:43
  110.5 1.9 %collective-permute-start.4 = (f32[1,1,16,5,128]{4,2,3,1,0:T(8,128)S(1)}, f32[1,1,16,5,128]{4,2,3,1,0:T(8,128)S(1)}, u32[]{:S(2)}, u32[]{:S(2)}) collective-permute-start(f32[1,1,16,5,128]{4,2,3,1,0:T(8,128)S(1)} %maximum_bitcast_fusion), channel_id=1, source_target_pairs={{0,4},{4,8},{8,12},{12,16},{16,20},{20,24},{24,28},{28,32},{32,36}... | collective-permute-start | bytes 122888 | tf_op jit(solution)/shard_map/ppermute | solution.py:41
  112.4 0.1 fusion.33
  112.5 0.0 collective-permute-done.5
  112.5 5.4 %collective-permute-done.4 = f32[1,1,16,5,128]{4,2,3,1,0:T(8,128)S(1)} collective-permute-done((f32[1,1,16,5,128]{4,2,3,1,0:T(8,128)S(1)}, f32[1,1,16,5,128]{4,2,3,1,0:T(8,128)S(1)}, u32[]{:S(2)}, u32[]{:S(2)}) %collective-permute-start.4) | collective-permute-done | bytes 40992 | tf_op jit(solution)/shard_map/ppermute | solution.py:41
  117.9 4.5 %collective-permute-start.7 = (f32[3,1,16,5,128]{4,2,3,1,0:T(8,128)S(1)}, f32[3,1,16,5,128]{4,2,3,1,0:T(8,128)S(1)}, u32[]{:S(2)}, u32[]{:S(2)}) collective-permute-start(f32[3,1,16,5,128]{4,2,3,1,0:T(8,128)S(1)} %pad_maximum_fusion.2), channel_id=1, source_target_pairs={{1,0},{2,1},{3,2},{5,4},{6,5},{7,6},{9,8},{10,9},{11,10},{13,12},{... | collective-permute-start | bytes 368648 | tf_op jit(solution)/shard_map/ppermute | solution.py:43
  122.4 1.9 %collective-permute-start.6 = (f32[3,1,16,5,128]{4,2,3,1,0:T(8,128)S(1)}, f32[3,1,16,5,128]{4,2,3,1,0:T(8,128)S(1)}, u32[]{:S(2)}, u32[]{:S(2)}) collective-permute-start(f32[3,1,16,5,128]{4,2,3,1,0:T(8,128)S(1)} %pad_maximum_fusion.2), channel_id=1, source_target_pairs={{0,1},{1,2},{2,3},{4,5},{5,6},{6,7},{8,9},{9,10},{10,11},{12,13},{... | collective-permute-start | bytes 368648 | tf_op jit(solution)/shard_map/ppermute | solution.py:41
  124.3 0.7 bitcast_select_fusion
  125.0 0.0 collective-permute-done.7
  125.0 4.2 %collective-permute-done.6 = f32[3,1,16,5,128]{4,2,3,1,0:T(8,128)S(1)} collective-permute-done((f32[3,1,16,5,128]{4,2,3,1,0:T(8,128)S(1)}, f32[3,1,16,5,128]{4,2,3,1,0:T(8,128)S(1)}, u32[]{:S(2)}, u32[]{:S(2)}) %collective-permute-start.6) | collective-permute-done | bytes 122912 | tf_op jit(solution)/shard_map/ppermute | solution.py:41
  129.3 0.1 copy.96
  129.4 0.7 gather_fusion.1
  130.1 0.1 fusion.50
  130.3 5.4 %fusion.5 = (f32[16,128]{1,0:T(8,128)S(1)}, f32[16,128]{1,0:T(8,128)S(1)}, f32[16,128]{1,0:T(8,128)S(1)}) fusion(f32[16,5,128]{2,1,0:T(8,128)S(1)} %bitcast.155, f32[16,128]{1,0:T(8,128)S(1)} %get-tuple-element.19, f32[16,128]{1,0:T(8,128)S(1)} %get-tuple-element.16, f32[16,5,128]{2,1,0:T(8,128)S(1)} %bitcast.157, f32[16,128]{1,0:T(8,128)S(1)} %get-tuple-element.20, ...), kind=kLoop, calls=%fused_computation.15 | loop fusion | flops 27518976 | bytes 270336 | tf_op jit(solution)/shard_map/reduce_sum | solution.py:67
  135.7 0.6 copy.129
  (26 shorter events, 0.3 us)
Async XLA Ops:
  0.6 2.2 %copy-start = (s32[8,4]{0,1:T(4,128)S(1)}, s32[8,4]{0,1:T(4,128)}, u32[]{:S(2)}) copy-start(s32[8,4]{0,1:T(4,128)} %param.14) | copy-start | bytes 388
  4.8 7.7 %all-to-all-start = ((s32[4,4,5]{2,1,0:T(4,128)}), s32[4,4,5]{2,1,0:T(4,128)S(1)}, u32[]{:S(2)}, u32[]{:S(2)}) async-start(s32[4,4,5]{2,1,0:T(4,128)} %copy.80), calls=%async_computation | async-start | bytes 16384 | tf_op jit(solution)/shard_map/all_to_all | solution.py:26
  12.5 8.7 %all-to-all-start.1 = ((f32[4,4,6,128]{3,1,2,0:T(4,128)}), f32[4,4,6,128]{3,1,2,0:T(4,128)S(1)}, u32[]{:S(2)}, u32[]{:S(2)}) async-start(f32[4,4,6,128]{3,1,2,0:T(4,128)} %fusion.10), calls=%async_computation.1 | async-start | bytes 98304 | tf_op jit(solution)/shard_map/all_to_all | solution.py:94
  21.2 64.3 %collective-permute-start.1 = (f32[1,1,16,4,128]{4,2,3,1,0:T(8,128)S(1)}, f32[1,1,16,4,128]{4,2,3,1,0:T(8,128)S(1)}, u32[]{:S(2)}, u32[]{:S(2)}) collective-permute-start(f32[1,1,16,4,128]{4,2,3,1,0:T(8,128)S(1)} %maximum_bitcast_fusion.1), channel_id=1, source_target_pairs={{4,0},{8,4},{12,8},{16,12},{20,16},{24,20},{28,24},{32,28},{36,32}... | collective-permute-start | bytes 98312 | tf_op jit(solution)/shard_map/ppermute | solution.py:43
  23.2 62.4 %collective-permute-start = (f32[1,1,16,4,128]{4,2,3,1,0:T(8,128)S(1)}, f32[1,1,16,4,128]{4,2,3,1,0:T(8,128)S(1)}, u32[]{:S(2)}, u32[]{:S(2)}) collective-permute-start(f32[1,1,16,4,128]{4,2,3,1,0:T(8,128)S(1)} %maximum_bitcast_fusion.1), channel_id=1, source_target_pairs={{0,4},{4,8},{8,12},{12,16},{16,20},{20,24},{24,28},{28,32},{32,36}... | collective-permute-start | bytes 98312 | tf_op jit(solution)/shard_map/ppermute | solution.py:41
  85.5 17.7 %collective-permute-start.3 = (f32[3,1,16,4,128]{4,2,3,1,0:T(8,128)S(1)}, f32[3,1,16,4,128]{4,2,3,1,0:T(8,128)S(1)}, u32[]{:S(2)}, u32[]{:S(2)}) collective-permute-start(f32[3,1,16,4,128]{4,2,3,1,0:T(8,128)S(1)} %pad_maximum_fusion.3), channel_id=1, source_target_pairs={{1,0},{2,1},{3,2},{5,4},{6,5},{7,6},{9,8},{10,9},{11,10},{13,12},{... | collective-permute-start | bytes 294920 | tf_op jit(solution)/shard_map/ppermute | solution.py:43
  89.0 14.2 %collective-permute-start.2 = (f32[3,1,16,4,128]{4,2,3,1,0:T(8,128)S(1)}, f32[3,1,16,4,128]{4,2,3,1,0:T(8,128)S(1)}, u32[]{:S(2)}, u32[]{:S(2)}) collective-permute-start(f32[3,1,16,4,128]{4,2,3,1,0:T(8,128)S(1)} %pad_maximum_fusion.3), channel_id=1, source_target_pairs={{0,1},{1,2},{2,3},{4,5},{5,6},{6,7},{8,9},{9,10},{10,11},{12,13},{... | collective-permute-start | bytes 294920 | tf_op jit(solution)/shard_map/ppermute | solution.py:41
  107.8 4.7 %collective-permute-start.5 = (f32[1,1,16,5,128]{4,2,3,1,0:T(8,128)S(1)}, f32[1,1,16,5,128]{4,2,3,1,0:T(8,128)S(1)}, u32[]{:S(2)}, u32[]{:S(2)}) collective-permute-start(f32[1,1,16,5,128]{4,2,3,1,0:T(8,128)S(1)} %maximum_bitcast_fusion), channel_id=1, source_target_pairs={{4,0},{8,4},{12,8},{16,12},{20,16},{24,20},{28,24},{32,28},{36,32}... | collective-permute-start | bytes 122888 | tf_op jit(solution)/shard_map/ppermute | solution.py:43
  110.5 7.4 %collective-permute-start.4 = (f32[1,1,16,5,128]{4,2,3,1,0:T(8,128)S(1)}, f32[1,1,16,5,128]{4,2,3,1,0:T(8,128)S(1)}, u32[]{:S(2)}, u32[]{:S(2)}) collective-permute-start(f32[1,1,16,5,128]{4,2,3,1,0:T(8,128)S(1)} %maximum_bitcast_fusion), channel_id=1, source_target_pairs={{0,4},{4,8},{8,12},{12,16},{16,20},{20,24},{24,28},{28,32},{32,36}... | collective-permute-start | bytes 122888 | tf_op jit(solution)/shard_map/ppermute | solution.py:41
  117.9 7.1 %collective-permute-start.7 = (f32[3,1,16,5,128]{4,2,3,1,0:T(8,128)S(1)}, f32[3,1,16,5,128]{4,2,3,1,0:T(8,128)S(1)}, u32[]{:S(2)}, u32[]{:S(2)}) collective-permute-start(f32[3,1,16,5,128]{4,2,3,1,0:T(8,128)S(1)} %pad_maximum_fusion.2), channel_id=1, source_target_pairs={{1,0},{2,1},{3,2},{5,4},{6,5},{7,6},{9,8},{10,9},{11,10},{13,12},{... | collective-permute-start | bytes 368648 | tf_op jit(solution)/shard_map/ppermute | solution.py:43
  122.4 6.8 %collective-permute-start.6 = (f32[3,1,16,5,128]{4,2,3,1,0:T(8,128)S(1)}, f32[3,1,16,5,128]{4,2,3,1,0:T(8,128)S(1)}, u32[]{:S(2)}, u32[]{:S(2)}) collective-permute-start(f32[3,1,16,5,128]{4,2,3,1,0:T(8,128)S(1)} %pad_maximum_fusion.2), channel_id=1, source_target_pairs={{0,1},{1,2},{2,3},{4,5},{5,6},{6,7},{8,9},{9,10},{10,11},{12,13},{... | collective-permute-start | bytes 368648 | tf_op jit(solution)/shard_map/ppermute | solution.py:41
where the time goes:
time: 137 us; the launch traced here: 136 us
  blocking collectives  71 us (52%)
  starting transfers between devices  31.6 us (23%)
  other arithmetic  13.4 us (10%)
  waiting for transfers between devices  12.7 us (9%)
  local copies, waits for them, and re-layouts  3.97 us (3%)
  matrix products  2.68 us (2%)
    pmin x4, blocking collectives, over_axes(): return functools.reduce(lax.pmin, axes, value)  71 us
    ppermute x4, starting transfers between devices, padded(): lax.ppermute(head, axis, [((i + 1) % count, i) for i in range(ends)])  12.6 us
    ppermute x4, waiting for transfers between devices, padded(): lax.ppermute(tail, axis, [(i, (i + 1) % count) for i in range(ends)])  9.57 us
    ppermute x4, starting transfers between devices, padded(): lax.ppermute(tail, axis, [(i, (i + 1) % count) for i in range(ends)])  8.59 us
    all_to_all x1, starting transfers between devices, body(): lax.all_to_all(send_fields.reshape(groups, CAP, 6, width), 'grp', split_a...  5.62 us
    reduce_sum x1, other arithmetic, partner_sums(): jnp.sum(coef * diffs[c], axis=(1, 3))  5.37 us
    all_to_all x1, starting transfers between devices, in_one_piece(): lax.all_to_all(both, axis, split_axis=split_dim, concat_axis=concat_dim,...  4.8 us
    reduce_sum x1, other arithmetic, partner_sums(): jnp.sum(part_m[:, :, None, :] * base ** 3, axis=(1, 3))  3.4 us
  transfers between devices with their start and end apart: 10, of which 4 were waited for; matrix products, arithmetic and copies ran while one was open for 3% of the time, Pallas kernels for 0%

commit v1 on v0

v1 whole, which is shorter than its diff:
```python
import functools
import math

import jax
import jax.numpy as jnp
from jax import lax
from jax.experimental import pallas as pl
from jax.experimental.pallas import tpu as pltpu
from jax.sharding import PartitionSpec as P

MESH = pl.DeviceIdType.MESH
CAP = 4
DRIFT = 0.05
GAMMA = 5.0 / 3.0
CFL = 0.3
KNORM = 315.0 / (64.0 * math.pi)

NB = 8
NG = 4
NZ, NY = 16, 8
W = 128
EMPTY = 12 * NB
CH = 32


def at(dom, grp):
    return {"dom": dom, "grp": grp}


def remote(src, dst, send, recv, to):
    return pltpu.make_async_remote_copy(
        src_ref=src, dst_ref=dst, send_sem=send, recv_sem=recv, device_id=to, device_id_type=MESH
    )


def landed(ref, sem):
    pltpu.make_async_copy(ref, ref, sem).wait()


def kernel(
    tgt, nbr, cnt, pos, vel, smooth, mass, energy, dens_out, acc_out, ts_out,
    pool, mfpool, table, rows, cols, coll, res, outsend, outbuf,
    mine, zbuf, ybuf, xbuf, ysrc, xsrc, last, final,
    dsend, drecv, tsend, trecv, fsend, frecv, osend, orecv, msend, mrecv,
):
    a = lax.axis_index("dom")
    g = lax.axis_index("grp")
    n_dom = lax.axis_size("dom")
    z, y, c = a // 16, (a // 2) % 8, a % 2
    root = z < 2
    low, high = a > 0, a < n_dom - 1

    def dom_of(zz, yy, cc):
        return (zz * NY + yy) * 2 + cc

    others = [lax.rem(g + d, NG) for d in (2, 1, 3)]
    y_peers = [at(dom_of(z, lax.rem(y + d, NY), c), g) for d in (4, 3, 5, 2, 6, 1, 7)]
    x_peers = [
        at(dom_of(z, y, lax.rem(c + dc, 2)), lax.rem(g + dx, NG))
        for dx in (2, 1, 3, 0) for dc in (0, 1) if dx or dc
    ]

    barrier = pltpu.get_barrier_semaphore()

    def greet(to):
        pl.semaphore_signal(barrier, inc=1, device_id=to, device_id_type=MESH)

    for o in others:
        greet(at(a, o))

    @pl.when(low)
    def _():
        greet(at(a - 1, g))

    @pl.when(high)
    def _():
        greet(at(a + 1, g))

    @pl.when(root)
    def _():
        def child(k, _):
            greet(at(dom_of(k, y, c), g))
            return 0

        lax.fori_loop(2, NZ, child, 0)
        greet(at(dom_of(1 - z, y, c), g))
        for p in y_peers + x_peers:
            greet(p)

    lane = lax.broadcasted_iota(jnp.int32, (NB, W), 1)
    sub = lax.broadcasted_iota(jnp.int32, (NB, W), 0)
    count = jnp.zeros((NB, W), jnp.int32)
    for b in range(NB):
        count = jnp.where(sub == b, cnt[b], count)
    active = lane < count
    h = smooth[...]
    u = energy[...]
    m = mass[...]
    steps = jnp.where(active, CFL * h / jnp.sqrt(GAMMA * (GAMMA - 1.0) * u), 1e30)
    mine[...] = jnp.min(steps, axis=0, keepdims=True)

    own = (NG + g) * 4 * NB
    for comp in range(3):
        for b in range(NB):
            piece = pl.ds(b * W, W)
            rows[comp * NB + b : comp * NB + b + 1, :] = (
                pos[comp : comp + 1, piece] + DRIFT * vel[comp : comp + 1, piece]
            )
        pool[pl.ds(pl.multiple_of(own + comp * NB, NB), NB), :] = rows[comp * NB : comp * NB + NB, :]
    pool[pl.ds(pl.multiple_of(own + 3 * NB, NB), NB), :] = m
    pool[pl.ds(EMPTY * 4, 4 * NB), :] = jnp.zeros((4 * NB, W), jnp.float32)
    mfpool[pl.ds(EMPTY, NB), :] = jnp.zeros((NB, W), jnp.float32)
    res[pl.ds(4 * NB, NB), :] = jnp.zeros((NB, W), jnp.float32)

    targets = [tgt[b] for b in range(NB)]
    ranks = []
    for b in range(NB):
        r = jnp.int32(0)
        for e in range(b):
            r = r + jnp.where(targets[e] == targets[b], 1, 0)
        ranks.append(r)
    places = [targets[b] * CAP + ranks[b] for b in range(NB)]
    for s in range(NG * CAP):
        found = jnp.int32(NB)
        for b in range(NB):
            found = jnp.where(places[b] == s, b, found)
        table[NG + g, s] = found

    @pl.when(jnp.logical_not(low))
    def _():
        for d in range(NG):
            for s in range(NG * CAP):
                table[d, s] = jnp.int32(NB)

    @pl.when(jnp.logical_not(high))
    def _():
        for d in range(NG):
            for s in range(NG * CAP):
                table[2 * NG + d, s] = jnp.int32(NB)

    wait_for = 3 + jnp.where(low, 1, 0) + jnp.where(high, 1, 0) + jnp.where(root, 15, 2)
    pl.semaphore_wait(barrier, wait_for)

    for zr in range(2):
        @pl.when(z != zr)
        def _():
            remote(mine, zbuf.at[pl.ds(z, 1)], msend.at[zr], mrecv.at[0], at(dom_of(zr, y, c), g)).start()

    def group_copies(ref, per, send, recv):
        part = ref.at[pl.ds(pl.multiple_of((NG + g) * per, per), per)]
        return [remote(part, part, send.at[k], recv.at[0], at(a, o)) for k, o in enumerate(others)]

    def side_copy(ref, per, send, recv, up):
        src = ref.at[pl.ds(NG * per, NG * per)]
        dst = ref.at[pl.ds(0 if up else 2 * NG * per, NG * per)]
        return remote(src, dst, send.at[3 if up else 4], recv.at[1 if up else 2], at(a + (1 if up else -1), g))

    def exchange(parts, between=None):
        for part in parts:
            for copy in group_copies(*part):
                copy.start()
        if between is not None:
            between()
        for ref, per, send, recv in parts:
            landed(ref.at[pl.ds(0, 3 * per)], recv.at[0])

        @pl.when(high)
        def _():
            for part in parts:
                side_copy(*part, True).start()

        @pl.when(low)
        def _():
            for part in parts:
                side_copy(*part, False).start()

    def arrived(parts):
        @pl.when(low)
        def _():
            for ref, per, send, recv in parts:
                landed(ref.at[pl.ds(0, NG * per)], recv.at[1])

        @pl.when(high)
        def _():
            for ref, per, send, recv in parts:
                landed(ref.at[pl.ds(0, NG * per)], recv.at[2])

    def sent(parts):
        for part in parts:
            for copy in group_copies(*part):
                copy.wait_send()

        @pl.when(high)
        def _():
            for part in parts:
                side_copy(*part, True).wait_send()

        @pl.when(low)
        def _():
            for part in parts:
                side_copy(*part, False).wait_send()

    first = ((pool, 4 * NB, dsend, drecv), (table, 1, tsend, trecv))
    second = ((mfpool, NB, fsend, frecv),)

    def columns():
        rows[3 * NB : 4 * NB, :] = h * h

        def one(b, _):
            for comp in range(4):
                row = rows[pl.ds(comp * NB + b, 1), :]
                cols[comp, pl.ds(pl.multiple_of(b * W, W), W), :] = jnp.transpose(jnp.broadcast_to(row, (W, W)))
            return 0

        lax.fori_loop(0, NB, one, 0)

    exchange(first, columns)
    arrived(first)

    def partner(b, k):
        if k == 0:
            return NG + g, b
        n = nbr[b * 4 + k - 1]
        cell, s = n // 16, n % 16
        i, j = cell // 3, cell % 3
        t = tgt[b] + j - 1
        d = i * NG + s // CAP
        e = table[d, jnp.clip(t, 0, NG - 1) * CAP + s % CAP]
        there = (t >= 0) & (t < NG) & (a + i >= 1) & (a + i <= n_dom) & (e < NB)
        return jnp.where(there, d, 3 * NG), jnp.where(there, e, 0)

    lane_of = lax.broadcasted_iota(jnp.int32, (CH, W), 1)

    def pairs(second_pass):
        def block(b, _):
            who = [partner(b, k) for k in range(5)]

            def chunk(q, _):
                mine_at = pl.ds(pl.multiple_of(b * W + q * CH, CH), CH)
                cx, cy, cz, ch2 = (cols[comp, mine_at, :] for comp in range(4))
                sums = [jnp.zeros((CH, W), jnp.float32) for _ in range(3 if second_pass else 4)]
                for d, e in who:
                    base = d * (4 * NB) + e
                    dx = cx - pool[pl.ds(base, 1), :]
                    dy = cy - pool[pl.ds(base + NB, 1), :]
                    dz = cz - pool[pl.ds(base + 2 * NB, 1), :]
                    w = jnp.maximum(ch2 - (dx * dx + dy * dy + dz * dz), 0.0)
                    if second_pass:
                        weight = mfpool[pl.ds(d * NB + e, 1), :]
                    else:
                        weight = pool[pl.ds(base + 3 * NB, 1), :]
                    mw = weight * (w * w)
                    parts = [mw * dx, mw * dy, mw * dz]
                    if not second_pass:
                        parts = parts + [mw * w]
                    sums = [s + p for s, p in zip(sums, parts)]
                here = pl.ds(pl.multiple_of(q * CH, CH), CH)
                kept = coll[here, :]
                for k, s in enumerate(sums):
                    kept = jnp.where(lane_of == k * NB + b, jnp.sum(s, axis=1, keepdims=True), kept)
                coll[here, :] = kept
                return 0

            lax.fori_loop(0, W // CH, chunk, 0)
            return 0

        coll[...] = jnp.zeros((W, W), jnp.float32)
        lax.fori_loop(0, NB, block, 0)
        return jnp.transpose(coll[...])

    inv_h = 1.0 / h
    ih3 = inv_h * inv_h * inv_h
    ih9 = KNORM * (ih3 * ih3 * ih3)

    found = pairs(False)
    rho = ih9 * found[3 * NB : 4 * NB, :]
    factor = (GAMMA - 1.0) * u / rho
    mfpool[pl.ds(pl.multiple_of((NG + g) * NB, NB), NB), :] = m * factor
    res[0:NB, :] = rho
    for comp in range(3):
        res[(1 + comp) * NB : (2 + comp) * NB, :] = factor * found[comp * NB : (comp + 1) * NB, :]

    exchange(second)
    arrived(second)

    found = pairs(True)
    for comp in range(3):
        here = slice((1 + comp) * NB, (2 + comp) * NB)
        total = 6.0 * ih9 * (res[here, :] + found[comp * NB : (comp + 1) * NB, :])
        res[here, :] = jnp.where(active, total, 0.0)

    for t in range(NG):
        for r in range(CAP):
            e = table[NG + g, t * CAP + r]
            for comp in range(4):
                source = jnp.where(e < NB, comp * NB + e, 4 * NB)
                outsend[t, comp * CAP + r : comp * CAP + r + 1, :] = res[pl.ds(source, 1), :]
    results = [remote(outsend.at[o], outbuf.at[g], osend.at[k], orecv, at(a, o)) for k, o in enumerate(others)]
    for copy in results:
        copy.start()
    outbuf[g] = outsend[g]
    landed(outbuf.at[pl.ds(0, 3)], orecv)
    for s in range(NG):
        dens_out[s * CAP : (s + 1) * CAP, :] = outbuf[s, 0:CAP, :]
        for comp in range(3):
            for r in range(CAP):
                row = (1 + comp) * CAP + r
                slot = s * CAP + r
                acc_out[comp : comp + 1, slot * W : (slot + 1) * W] = outbuf[s, row : row + 1, :]

    def reduce_and_send(buf, index, value, src, peers, send, recv, slot):
        buf[pl.ds(index, 1), :] = value
        src[...] = value
        for k, p in enumerate(peers):
            remote(src, buf.at[pl.ds(index, 1)], send.at[k], recv, p).start()
        landed(buf.at[pl.ds(0, slot - 1)], recv)
        return jnp.min(buf[...], axis=0, keepdims=True)

    @pl.when(root)
    def _():
        zbuf[pl.ds(z, 1), :] = mine[...]
        landed(zbuf.at[pl.ds(0, NZ - 1)], mrecv.at[0])
        least = jnp.min(zbuf[...], axis=0, keepdims=True)
        least = reduce_and_send(ybuf, y, least, ysrc, y_peers, msend.at[pl.ds(2, 7)], mrecv.at[1], NY)
        least = reduce_and_send(xbuf, c * NG + g, least, xsrc, x_peers, msend.at[pl.ds(9, 7)], mrecv.at[2], 2 * NG)
        last[...] = least

        def child(k, _):
            to = jnp.where(z == 0, NZ - 1 - k, 2 + k)
            remote(last, final, msend.at[16 + k], mrecv.at[3], at(dom_of(to, y, c), g)).start()
            return 0

        lax.fori_loop(0, 7, child, 0)
        final[...] = least
        for k in range(21):
            landed(last, msend.at[2 + k])

    @pl.when(jnp.logical_not(root))
    def _():
        landed(final, mrecv.at[3])

    ts_out[...] = jnp.broadcast_to(jnp.min(final[...], axis=1, keepdims=True), (1, W))

    sent(first)
    sent(second)
    for copy in results:
        copy.wait_send()
    for zr in range(2):
        @pl.when(z != zr)
        def _():
            landed(mine, msend.at[zr])


def body(positions, velocity, smoothing, mass, energy, targets, neighbours, counts):
    f32 = jnp.float32
    slots = NG * CAP
    vmem, smem = pl.BlockSpec(memory_space=pltpu.VMEM), pl.BlockSpec(memory_space=pltpu.SMEM)
    sem = pltpu.SemaphoreType.DMA
    dens, acc, ts = pl.pallas_call(
        kernel,
        out_shape=(
            jax.ShapeDtypeStruct((slots, W), f32),
            jax.ShapeDtypeStruct((3, slots * W), f32),
            jax.ShapeDtypeStruct((1, W), f32),
        ),
        in_specs=[smem] * 3 + [vmem] * 5,
        out_specs=(vmem, vmem, vmem),
        scratch_shapes=[
            pltpu.VMEM(((EMPTY + NB) * 4, W), f32),
            pltpu.VMEM((EMPTY + NB, W), f32),
            pltpu.SMEM((3 * NG, 16), jnp.int32),
            pltpu.VMEM((4 * NB, W), f32),
            pltpu.VMEM((4, NB * W, W), f32),
            pltpu.VMEM((W, W), f32),
            pltpu.VMEM((5 * NB, W), f32),
            pltpu.VMEM((NG, 4 * CAP, W), f32),
            pltpu.VMEM((NG, 4 * CAP, W), f32),
            pltpu.VMEM((1, W), f32),
            pltpu.VMEM((NZ, W), f32),
            pltpu.VMEM((NY, W), f32),
            pltpu.VMEM((2 * NG, W), f32),
            pltpu.VMEM((1, W), f32),
            pltpu.VMEM((1, W), f32),
            pltpu.VMEM((1, W), f32),
            pltpu.VMEM((1, W), f32),
            sem((5,)), sem((3,)), sem((5,)), sem((3,)), sem((5,)), sem((3,)),
            sem((3,)), sem, sem((24,)), sem((4,)),
        ],
        compiler_params=pltpu.CompilerParams(collective_id=0, has_side_effects=True),
    )(
        targets.reshape(-1), neighbours.reshape(-1), counts, positions, velocity,
        smoothing.reshape(NB, W), mass.reshape(NB, W), energy.reshape(NB, W),
    )
    return dens.reshape(-1), acc, ts[0, :1]


def solution(mesh):
    both = ("dom", "grp")
    return jax.shard_map(
        body,
        mesh=mesh,
        in_specs=(P(None, both), P(None, both), P(both), P(both), P(both), P(both, None), P(both, None), P(both)),
        out_specs=(P(both), P(None, both), P()),
        check_vma=False,
    )
```

time: 137 us -> 60.6 us (0.44)
  the two profiles are of different devices: /device:TPU:68 before, /device:TPU:1 now
where the time goes in v1:
time: 60.6 us; the launch traced here: 60.2 us
  Pallas kernels  54.4 us (90%)
  local copies, waits for them, and re-layouts  4.02 us (7%)
  between operations  1.82 us (3%)
    pallas_call x1, Pallas kernels, body(): pl.pallas_call(kernel, out_shape=(jax.ShapeDtypeStruct((slots, W), f32),...  54.4 us
    unnamed x9, local copies, waits for them, and re-layouts  3.43 us

profile of v1, /device:TPU:1, one launch (start us, length us, event | category | flops | bytes accessed | tf_op | source)
XLA Modules:
  0.0 60.2 jit_solution(17325300509956708675)
XLA Ops:
  0.6 0.0 copy-start.1
  0.6 0.7 %copy-done.1 = s32[8,4]{0,1:T(4,128)S(1)} copy-done((s32[8,4]{0,1:T(4,128)S(1)}, s32[8,4]{0,1:T(4,128)}, u32[]{:S(2)}) %copy-start.1) | copy-done | bytes 152
  1.3 0.1 copy.12
  1.4 0.6 reshape.25.nbr
  2.0 54.4 %shard_map.103 = (f32[16,128]{1,0:T(8,128)}, f32[3,2048]{1,0:T(4,128)}, f32[1,128]{1,0:T(1,128)}) custom-call(s32[8]{0:T(128)} %bitcast.11, s32[32]{0:T(128)} %reshape.25.nbr, s32[8]{0:T(128)} %cnt.1, f32[3,1024]{1,0:T(4,128)} %pos.1, f32[3,1024]{1,0:T(4,128)} %vel.1, f32[8,128]{1,0:T(8,128)} %bitcast.8, f32[8,128]{1,0:T(8,128)} %bitcast.9, f32[8,128]{1,0:T(8,128)} %bitcast.10), custom_call_target="tpu_custom_call" | custom-call | tf_op jit(solution)/shard_map/pallas_call | solution.py:359
  56.4 0.0 copy-start
  56.4 0.7 %copy-done = f32[16,128]{1,0:T(8,128)S(1)} copy-done((f32[16,128]{1,0:T(8,128)S(1)}, f32[16,128]{1,0:T(8,128)}, u32[]{:S(2)}) %copy-start) | copy-done | bytes 8216
  57.1 0.6 copy.16
  57.7 0.0 copy-start.2
  57.7 1.4 %copy.17 = f32[3,2048]{1,0:T(4,128)} copy(f32[3,2048]{1,0:T(4,128)} %get-tuple-element.13) | data formatting | bytes 49152
  59.1 0.0 copy-done.2
Async XLA Ops:
  0.6 0.7 %copy-start.1 = (s32[8,4]{0,1:T(4,128)S(1)}, s32[8,4]{0,1:T(4,128)}, u32[]{:S(2)}) copy-start(s32[8,4]{0,1:T(4,128)} %param.14) | copy-start | bytes 388
  56.4 0.7 %copy-start = (f32[16,128]{1,0:T(8,128)S(1)}, f32[16,128]{1,0:T(8,128)}, u32[]{:S(2)}) copy-start(f32[16,128]{1,0:T(8,128)} %get-tuple-element.6) | copy-start | bytes 24580
  57.7 1.4 %copy-start.2 = (f32[1,128]{1,0:T(1,128)S(1)}, f32[1,128]{1,0:T(1,128)}, u32[]{:S(2)}) copy-start(f32[1,128]{1,0:T(1,128)} %get-tuple-element.8) | copy-start | bytes 1540

commit v2 on v1

v2 whole, which is shorter than its diff:
```python
import functools
import math

import jax
import jax.numpy as jnp
from jax import lax
from jax.experimental import pallas as pl
from jax.experimental.pallas import tpu as pltpu
from jax.sharding import PartitionSpec as P

MESH = pl.DeviceIdType.MESH
CAP = 4
DRIFT = 0.05
GAMMA = 5.0 / 3.0
CFL = 0.3
KNORM = 315.0 / (64.0 * math.pi)

NB = 8
NG = 4
NZ, NY = 16, 8
W = 128
EMPTY = 12 * NB
CH = 32


def at(dom, grp):
    return {"dom": dom, "grp": grp}


def remote(src, dst, send, recv, to):
    return pltpu.make_async_remote_copy(
        src_ref=src, dst_ref=dst, send_sem=send, recv_sem=recv, device_id=to, device_id_type=MESH
    )


def landed(ref, sem):
    pltpu.make_async_copy(ref, ref, sem).wait()


def kernel(
    tgt_in, nbr_in, cnt_in, pos_in, vel_in, smooth_in, mass_in, energy_in, slots_out, least_out,
    tgt, nbr, cnt, pos, vel, smooth, mass, energy, base_of,
    pool, mfpool, table, rows, cols, stash, coll, res, outsend, outbuf,
    mine, zbuf, xbuf, last, final,
    load, dsend, drecv, tsend, trecv, fsend, frecv, osend, orecv, msend, mrecv,
):
    a = lax.axis_index("dom")
    g = lax.axis_index("grp")
    n_dom = lax.axis_size("dom")
    z, y, c = a // 16, (a // 2) % 8, a % 2
    root = z < 2
    low, high = a > 0, a < n_dom - 1

    def dom_of(zz, yy, cc):
        return (zz * NY + yy) * 2 + cc

    others = [lax.rem(g + d, NG) for d in (2, 1, 3)]
    plane = [
        at(dom_of(z, lax.rem(y + dy, NY), lax.rem(c + dc, 2)), lax.rem(g + dx, NG))
        for dy in (4, 3, 5, 2, 6, 1, 7, 0) for dx in (2, 1, 3, 0) for dc in (0, 1) if dy or dx or dc
    ]

    loads = [
        pltpu.make_async_copy(src, dst, load.at[k])
        for k, (src, dst) in enumerate((
            (cnt_in, cnt), (smooth_in, smooth), (energy_in, energy), (tgt_in, tgt),
            (pos_in, pos), (vel_in, vel), (mass_in, mass), (nbr_in, nbr),
        ))
    ]
    for copy in loads:
        copy.start()

    barrier = pltpu.get_barrier_semaphore()

    def greet(to):
        pl.semaphore_signal(barrier, inc=1, device_id=to, device_id_type=MESH)

    for o in others:
        greet(at(a, o))

    @pl.when(low)
    def _():
        greet(at(a - 1, g))

    @pl.when(high)
    def _():
        greet(at(a + 1, g))

    @pl.when(root)
    def _():
        def child(k, _):
            greet(at(dom_of(k, y, c), g))
            return 0

        lax.fori_loop(2, NZ, child, 0)
        greet(at(dom_of(1 - z, y, c), g))
        for p in plane:
            greet(p)

    lane = lax.broadcasted_iota(jnp.int32, (NB, W), 1)
    sub = lax.broadcasted_iota(jnp.int32, (NB, W), 0)
    for copy in loads[:3]:
        copy.wait()
    count = jnp.zeros((NB, W), jnp.int32)
    for b in range(NB):
        count = jnp.where(sub == b, cnt[b], count)
    active = lane < count
    h = smooth[...]
    u = energy[...]
    steps = jnp.where(active, CFL * h / jnp.sqrt(GAMMA * (GAMMA - 1.0) * u), 1e30)
    mine[...] = jnp.min(steps, axis=0, keepdims=True)

    wait_for = 3 + jnp.where(low, 1, 0) + jnp.where(high, 1, 0) + jnp.where(root, len(plane) + 1, 2)
    pl.semaphore_wait(barrier, wait_for)

    for zr in range(2):
        @pl.when(z != zr)
        def _():
            remote(mine, zbuf.at[pl.ds(z, 1)], msend.at[zr], mrecv.at[0], at(dom_of(zr, y, c), g)).start()

    for copy in loads[3:]:
        copy.wait()
    m = mass[...]

    own = (NG + g) * 4 * NB
    for comp in range(3):
        for b in range(NB):
            piece = pl.ds(b * W, W)
            rows[comp * NB + b : comp * NB + b + 1, :] = (
                pos[comp : comp + 1, piece] + DRIFT * vel[comp : comp + 1, piece]
            )
        pool[pl.ds(pl.multiple_of(own + comp * NB, NB), NB), :] = rows[comp * NB : comp * NB + NB, :]
    pool[pl.ds(pl.multiple_of(own + 3 * NB, NB), NB), :] = m
    pool[pl.ds(EMPTY * 4, 4 * NB), :] = jnp.zeros((4 * NB, W), jnp.float32)
    mfpool[pl.ds(EMPTY, NB), :] = jnp.zeros((NB, W), jnp.float32)
    res[pl.ds(4 * NB, NB), :] = jnp.zeros((NB, W), jnp.float32)

    targets = [tgt[b] for b in range(NB)]
    ranks = []
    for b in range(NB):
        r = jnp.int32(0)
        for e in range(b):
            r = r + jnp.where(targets[e] == targets[b], 1, 0)
        ranks.append(r)
    places = [targets[b] * CAP + ranks[b] for b in range(NB)]
    for s in range(NG * CAP):
        found = jnp.int32(NB)
        for b in range(NB):
            found = jnp.where(places[b] == s, b, found)
        table[NG + g, s] = found

    @pl.when(jnp.logical_not(low))
    def _():
        for d in range(NG):
            for s in range(NG * CAP):
                table[d, s] = jnp.int32(NB)

    @pl.when(jnp.logical_not(high))
    def _():
        for d in range(NG):
            for s in range(NG * CAP):
                table[2 * NG + d, s] = jnp.int32(NB)

    def piece_at(ref, per, i, d):
        return ref.at[pl.ds(pl.multiple_of((i * NG + lax.rem(g + d, NG)) * per, per), per)]

    def over_group(ref, per, send, recv, d):
        part = piece_at(ref, per, 1, 0)
        return remote(part, part, send.at[d], recv.at[NG - d], at(a, lax.rem(g + d, NG)))

    def to_side(ref, per, send, recv, d, up):
        src, dst = piece_at(ref, per, 1, d), piece_at(ref, per, 0 if up else 2, d)
        k = NG if up else NG + 1
        return remote(src, dst, send.at[(k - 3) * NG + d], recv.at[k], at(a + (1 if up else -1), g))

    def sides(parts, d, do):
        for up, there in ((True, high), (False, low)):
            @pl.when(there)
            def _():
                for part in parts:
                    do(to_side(*part, d, up))

    def gathered(parts, between):
        for d in (2, 1, 3):
            for part in parts:
                over_group(*part, d).start()
        sides(parts, 0, lambda copy: copy.start())
        between()
        for d in (1, 3, 2):
            for ref, per, send, recv in parts:
                landed(ref.at[pl.ds(0, per)], recv.at[d])
            sides(parts, d, lambda copy: copy.start())
        for k, there in ((NG, low), (NG + 1, high)):
            @pl.when(there)
            def _():
                for ref, per, send, recv in parts:
                    landed(ref.at[pl.ds(0, NG * per)], recv.at[k])

    def sent(parts):
        for d in (2, 1, 3):
            for part in parts:
                over_group(*part, d).wait_send()
        for d in range(NG):
            sides(parts, d, lambda copy: copy.wait_send())

    first = ((pool, 4 * NB, dsend, drecv), (table, 1, tsend, trecv))

    def columns():
        rows[3 * NB : 4 * NB, :] = h * h

        def one(b, _):
            for comp in range(4):
                row = rows[pl.ds(comp * NB + b, 1), :]
                cols[comp, pl.ds(pl.multiple_of(b * W, W), W), :] = jnp.transpose(jnp.broadcast_to(row, (W, W)))
            return 0

        lax.fori_loop(0, NB, one, 0)

    gathered(first, columns)

    def partner(b, k):
        if k == 0:
            return NG + g, b
        n = nbr[k - 1, b]
        cell, s = n // 16, n % 16
        i, j = cell // 3, cell % 3
        t = tgt[b] + j - 1
        d = i * NG + s // CAP
        e = table[d, jnp.clip(t, 0, NG - 1) * CAP + s % CAP]
        there = (t >= 0) & (t < NG) & (a + i >= 1) & (a + i <= n_dom) & (e < NB)
        return jnp.where(there, d, 3 * NG), jnp.where(there, e, 0)

    def find(b):
        who = [partner(b, k) for k in range(5)]
        for k, (d, e) in enumerate(who):
            base_of[b * 5 + k] = d * NB + e
        return who

    lane_of = lax.broadcasted_iota(jnp.int32, (CH, W), 1)

    def keep(q, b, sums):
        here = slice(q * CH, (q + 1) * CH)
        kept = coll[here, :]
        for k, s in enumerate(sums):
            kept = jnp.where(lane_of == k * NB + b, jnp.sum(s, axis=1, keepdims=True), kept)
        coll[here, :] = kept

    def stashed(b, k, q):
        return pl.ds(pl.multiple_of((b * 5 + k) * W + q * CH, CH), CH)

    def density_pairs(b, _):
        who = find(b)
        for q in range(W // CH):
            mine_at = pl.ds(pl.multiple_of(b * W + q * CH, CH), CH)
            cx, cy, cz, ch2 = (cols[comp, mine_at, :] for comp in range(4))
            sums = [jnp.zeros((CH, W), jnp.float32) for _ in range(4)]
            for k, (d, e) in enumerate(who):
                base = d * (4 * NB) + e
                dx = cx - pool[pl.ds(base, 1), :]
                dy = cy - pool[pl.ds(base + NB, 1), :]
                dz = cz - pool[pl.ds(base + 2 * NB, 1), :]
                w = jnp.maximum(ch2 - (dx * dx + dy * dy + dz * dz), 0.0)
                w2 = w * w
                m_j = pool[pl.ds(base + 3 * NB, 1), :]
                parts = []
                for comp, delta in enumerate((dx, dy, dz)):
                    part = w2 * delta
                    stash[comp, stashed(b, k, q), :] = part
                    parts.append(m_j * part)
                parts.append(m_j * (w2 * w))
                sums = [s + p for s, p in zip(sums, parts)]
            keep(q, b, sums)
        return 0

    def force_pairs(b, _):
        who = [base_of[b * 5 + k] for k in range(5)]
        for q in range(W // CH):
            sums = [jnp.zeros((CH, W), jnp.float32) for _ in range(3)]
            for k, base in enumerate(who):
                mf_j = mfpool[pl.ds(base, 1), :]
                sums = [s + mf_j * stash[comp, stashed(b, k, q), :] for comp, s in enumerate(sums)]
            keep(q, b, sums)
        return 0

    def pairs(block):
        coll[...] = jnp.zeros((W, W), jnp.float32)
        lax.fori_loop(0, NB, block, 0)
        return jnp.transpose(coll[...])

    inv_h = 1.0 / h
    ih3 = inv_h * inv_h * inv_h
    ih9 = KNORM * (ih3 * ih3 * ih3)

    found = pairs(density_pairs)
    rho = ih9 * found[3 * NB : 4 * NB, :]
    factor = (GAMMA - 1.0) * u / rho
    mfpool[pl.ds(pl.multiple_of((NG + g) * NB, NB), NB), :] = m * factor
    res[0:NB, :] = rho
    for comp in range(3):
        res[(1 + comp) * NB : (2 + comp) * NB, :] = factor * found[comp * NB : (comp + 1) * NB, :]

    part = mfpool.at[pl.ds(pl.multiple_of((NG + g) * NB, NB), NB)]

    def factors(i):
        dst = mfpool.at[pl.ds(pl.multiple_of(((1 - i) * NG + g) * NB, NB), NB)]
        to = others if i == 0 else others + [g]
        return [
            remote(part, dst, fsend.at[(i + 1) * NG + k], frecv.at[1 - i], at(a + i, o)) for k, o in enumerate(to)
        ]

    def on_sides(do):
        for i, there in ((1, high), (-1, low)):
            pl.when(there)(functools.partial(do, i))

    def start_factors(i):
        for copy in factors(i):
            copy.start()

    def sent_factors(i):
        for copy in factors(i):
            copy.wait_send()

    on_sides(start_factors)
    start_factors(0)
    landed(mfpool.at[pl.ds(0, 3 * NB)], frecv.at[1])
    on_sides(lambda i: landed(mfpool.at[pl.ds(0, NG * NB)], frecv.at[1 + i]))

    found = pairs(force_pairs)
    for comp in range(3):
        here = slice((1 + comp) * NB, (2 + comp) * NB)
        total = 6.0 * ih9 * (res[here, :] + found[comp * NB : (comp + 1) * NB, :])
        res[here, :] = jnp.where(active, total, 0.0)

    for t in range(NG):
        for r in range(CAP):
            e = table[NG + g, t * CAP + r]
            for comp in range(4):
                source = jnp.where(e < NB, comp * NB + e, 4 * NB)
                outsend[t, comp * CAP + r : comp * CAP + r + 1, :] = res[pl.ds(source, 1), :]
    results = [remote(outsend.at[o], outbuf.at[g], osend.at[k], orecv, at(a, o)) for k, o in enumerate(others)]
    for copy in results:
        copy.start()
    outbuf[g] = outsend[g]

    @pl.when(root)
    def _():
        zbuf[pl.ds(z, 1), :] = mine[...]
        landed(zbuf.at[pl.ds(0, NZ - 1)], mrecv.at[0])
        least = jnp.min(zbuf[...], axis=0, keepdims=True)
        index = (y * 2 + c) * NG + g
        last[...] = least
        xbuf[pl.ds(index, 1), :] = least
        for k, p in enumerate(plane):
            remote(last, xbuf.at[pl.ds(index, 1)], msend.at[2 + k], mrecv.at[1], p).start()

    landed(outbuf.at[pl.ds(0, 3)], orecv)
    slots_out[...] = outbuf[...]

    @pl.when(root)
    def _():
        landed(xbuf.at[pl.ds(0, len(plane))], mrecv.at[1])
        final[...] = jnp.min(xbuf[...], axis=0, keepdims=True)

        def child(k, _):
            to = jnp.where(z == 0, NZ - 1 - k, 2 + k)
            remote(final, final, msend.at[2 + len(plane) + k], mrecv.at[2], at(dom_of(to, y, c), g)).start()
            return 0

        lax.fori_loop(0, 7, child, 0)

    @pl.when(jnp.logical_not(root))
    def _():
        landed(final, mrecv.at[2])

    least_out[...] = final[...]

    sent(first)
    sent_factors(0)
    on_sides(sent_factors)
    for copy in results:
        copy.wait_send()
    for zr in range(2):
        @pl.when(z != zr)
        def _():
            landed(mine, msend.at[zr])

    @pl.when(root)
    def _():
        for k in range(len(plane) + 7):
            landed(last, msend.at[2 + k])


def unpack(slots_in, least_in, dens_out, acc_out, ts_out):
    for s in range(NG):
        dens_out[s * CAP : (s + 1) * CAP, :] = slots_in[s, 0:CAP, :]
        for comp in range(3):
            for r in range(CAP):
                row = (1 + comp) * CAP + r
                slot = s * CAP + r
                acc_out[comp : comp + 1, slot * W : (slot + 1) * W] = slots_in[s, row : row + 1, :]
    ts_out[0] = jnp.min(least_in[...])


def body(positions, velocity, smoothing, mass, energy, targets, neighbours, counts):
    f32 = jnp.float32
    slots = NG * CAP
    vmem, smem = pl.BlockSpec(memory_space=pltpu.VMEM), pl.BlockSpec(memory_space=pltpu.SMEM)
    sem = pltpu.SemaphoreType.DMA
    packed, least = pl.pallas_call(
        kernel,
        out_shape=(pltpu.VMEM((NG, 4 * CAP, W), f32), pltpu.VMEM((1, W), f32)),
        in_specs=[pl.BlockSpec(memory_space=pl.ANY)] * 8,
        out_specs=(vmem, vmem),
        scratch_shapes=[
            pltpu.SMEM((NB,), jnp.int32),
            pltpu.SMEM((4, NB), jnp.int32),
            pltpu.SMEM((NB,), jnp.int32),
            pltpu.VMEM((3, NB * W), f32),
            pltpu.VMEM((3, NB * W), f32),
            pltpu.VMEM((NB, W), f32),
            pltpu.VMEM((NB, W), f32),
            pltpu.VMEM((NB, W), f32),
            pltpu.SMEM((5 * NB,), jnp.int32),
            pltpu.VMEM(((EMPTY + NB) * 4, W), f32),
            pltpu.VMEM((EMPTY + NB, W), f32),
            pltpu.SMEM((3 * NG, 16), jnp.int32),
            pltpu.VMEM((4 * NB, W), f32),
            pltpu.VMEM((4, NB * W, W), f32),
            pltpu.VMEM((3, 5 * NB * W, W), f32),
            pltpu.VMEM((W, W), f32),
            pltpu.VMEM((5 * NB, W), f32),
            pltpu.VMEM((NG, 4 * CAP, W), f32),
            pltpu.VMEM((NG, 4 * CAP, W), f32),
            pltpu.VMEM((1, W), f32),
            pltpu.VMEM((NZ, W), f32),
            pltpu.VMEM((2 * NY * NG, W), f32),
            pltpu.VMEM((1, W), f32),
            pltpu.VMEM((1, W), f32),
            sem((8,)), sem((3 * NG,)), sem((6,)), sem((3 * NG,)), sem((6,)), sem((3 * NG,)), sem((3,)),
            sem((3,)), sem, sem((2 + 63 + 7,)), sem((3,)),
        ],
        compiler_params=pltpu.CompilerParams(collective_id=0, has_side_effects=True),
    )(
        targets.reshape(-1), neighbours.T, counts, positions, velocity,
        smoothing.reshape(NB, W), mass.reshape(NB, W), energy.reshape(NB, W),
    )
    dens, acc, ts = pl.pallas_call(
        unpack,
        out_shape=(
            jax.ShapeDtypeStruct((slots, W), f32),
            jax.ShapeDtypeStruct((3, slots * W), f32),
            jax.ShapeDtypeStruct((1,), f32),
        ),
        in_specs=[vmem] * 2,
        out_specs=(vmem, vmem, smem),
    )(*(pltpu.with_memory_space_constraint(v, pltpu.VMEM) for v in (packed, least)))
    return dens.reshape(-1), acc, ts


def solution(mesh):
    both = ("dom", "grp")
    return jax.shard_map(
        body,
        mesh=mesh,
        in_specs=(P(None, both), P(None, both), P(both), P(both), P(both), P(both, None), P(both, None), P(both)),
        out_specs=(P(both), P(None, both), P()),
        check_vma=False,
    )
```

time: 60.6 us -> 43.8 us (0.72)
  Pallas kernels: 54.4 us -> 42.9 us
  local copies, waits for them, and re-layouts: 4.02 us -> 0 us
  between operations: 1.82 us -> 0.64 us
    pallas_call x1 -> x2, Pallas kernels: 54.4 us -> 42.9 us  [the longest x1 42.3 us: body(): pl.pallas_call(kernel, out_shape=(pltpu.VMEM((NG, 4 * CAP, W), f32), pltp...]
    unnamed x9 -> x0, local copies, waits for them, and re-layouts: 3.43 us -> none
where the time goes in v2:
time: 43.8 us; the launch traced here: 43.6 us
  Pallas kernels  42.9 us (98%)
  between operations  0.64 us (1%)
    pallas_call x1, Pallas kernels, body(): pl.pallas_call(kernel, out_shape=(pltpu.VMEM((NG, 4 * CAP, W), f32), pltp...  42.3 us

profile of v2, /device:TPU:1, one launch (start us, length us, event | category | flops | bytes accessed | tf_op | source)
XLA Modules:
  0.0 43.6 jit_solution(12309301027029119385)
XLA Ops:
  0.6 42.3 %shard_map.103 = (f32[4,16,128]{2,1,0:T(8,128)S(1)}, f32[1,128]{1,0:T(1,128)S(1)}) custom-call(s32[8]{0:T(128)} %bitcast.10, s32[4,8]{1,0:T(4,128)} %bitcast.9, s32[8]{0:T(128)} %cnt_in.1, f32[3,1024]{1,0:T(4,128)} %pos_in.1, f32[3,1024]{1,0:T(4,128)} %vel_in.1, f32[8,128]{1,0:T(8,128)} %bitcast.6, f32[8,128]{1,0:T(8,128)} %bitcast.7, f32[8,128]{1,0:T(8,128)} %bitcast.8), custom_call_target="tpu_custom_call" | custom-call | tf_op jit(solution)/shard_map/pallas_call | solution.py:409
  42.9 0.6 %shard_map.104 = (f32[16,128]{1,0:T(8,128)}, f32[3,2048]{1,0:T(4,128)}, f32[1]{0:T(128)}) custom-call(f32[4,16,128]{2,1,0:T(8,128)S(1)} %get-tuple-element.8.slots_in, f32[1,128]{1,0:T(1,128)S(1)} %get-tuple-element.9.least_in), custom_call_target="tpu_custom_call" | custom-call | tf_op jit(solution)/shard_map/pallas_call | solution.py:447

commit v3 on v2

--- a/solution.py
+++ b/solution.py
@@ -21,6 +21,7 @@
 W = 128
 EMPTY = 12 * NB
 CH = 32
+ROOTS = (1, 2)
 
 
 def at(dom, grp):
@@ -48,7 +49,7 @@
     g = lax.axis_index("grp")
     n_dom = lax.axis_size("dom")
     z, y, c = a // 16, (a // 2) % 8, a % 2
-    root = z < 2
+    root = (z == ROOTS[0]) | (z == ROOTS[1])
     low, high = a > 0, a < n_dom - 1
 
     def dom_of(zz, yy, cc):
@@ -89,11 +90,11 @@
     @pl.when(root)
     def _():
         def child(k, _):
-            greet(at(dom_of(k, y, c), g))
+            greet(at(dom_of(lax.rem(ROOTS[1] + 1 + k, NZ), y, c), g))
             return 0
 
-        lax.fori_loop(2, NZ, child, 0)
-        greet(at(dom_of(1 - z, y, c), g))
+        lax.fori_loop(0, NZ - 2, child, 0)
+        greet(at(dom_of(ROOTS[0] + ROOTS[1] - z, y, c), g))
         for p in plane:
             greet(p)
 
@@ -113,10 +114,10 @@
     wait_for = 3 + jnp.where(low, 1, 0) + jnp.where(high, 1, 0) + jnp.where(root, len(plane) + 1, 2)
     pl.semaphore_wait(barrier, wait_for)
 
-    for zr in range(2):
+    for k, zr in enumerate(ROOTS):
         @pl.when(z != zr)
         def _():
-            remote(mine, zbuf.at[pl.ds(z, 1)], msend.at[zr], mrecv.at[0], at(dom_of(zr, y, c), g)).start()
+            remote(mine, zbuf.at[pl.ds(z, 1)], msend.at[k], mrecv.at[0], at(dom_of(zr, y, c), g)).start()
 
     for copy in loads[3:]:
         copy.wait()
@@ -362,7 +363,7 @@
         final[...] = jnp.min(xbuf[...], axis=0, keepdims=True)
 
         def child(k, _):
-            to = jnp.where(z == 0, NZ - 1 - k, 2 + k)
+            to = jnp.where(z == ROOTS[0], lax.rem(ROOTS[0] + NZ - 1 - k, NZ), lax.rem(ROOTS[1] + 1 + k, NZ))
             remote(final, final, msend.at[2 + len(plane) + k], mrecv.at[2], at(dom_of(to, y, c), g)).start()
             return 0
 
@@ -379,10 +380,10 @@
     on_sides(sent_factors)
     for copy in results:
         copy.wait_send()
-    for zr in range(2):
+    for k, zr in enumerate(ROOTS):
         @pl.when(z != zr)
         def _():
-            landed(mine, msend.at[zr])
+            landed(mine, msend.at[k])
 
     @pl.when(root)
     def _():

time: 43.8 us -> 37.8 us (0.86)
  Pallas kernels: 42.9 us -> 37 us
    pallas_call x1, Pallas kernels: 42.3 us -> 36.3 us  [body(): pl.pallas_call(kernel, out_shape=(pltpu.VMEM((NG, 4 * CAP, W), f32), pltp...]
where the time goes in v3:
time: 37.8 us; the launch traced here: 37.6 us
  Pallas kernels  37 us (98%)
  between operations  0.64 us (2%)
    pallas_call x1, Pallas kernels, body(): pl.pallas_call(kernel, out_shape=(pltpu.VMEM((NG, 4 * CAP, W), f32), pltp...  36.3 us

profile of v3, /device:TPU:1, one launch (start us, length us, event | category | flops | bytes accessed | tf_op | source)
XLA Modules:
  0.0 37.6 jit_solution(1225699438235323089)
XLA Ops:
  0.6 36.3 %shard_map.103 = (f32[4,16,128]{2,1,0:T(8,128)S(1)}, f32[1,128]{1,0:T(1,128)S(1)}) custom-call(s32[8]{0:T(128)} %bitcast.10, s32[4,8]{1,0:T(4,128)} %bitcast.9, s32[8]{0:T(128)} %cnt_in.1, f32[3,1024]{1,0:T(4,128)} %pos_in.1, f32[3,1024]{1,0:T(4,128)} %vel_in.1, f32[8,128]{1,0:T(8,128)} %bitcast.6, f32[8,128]{1,0:T(8,128)} %bitcast.7, f32[8,128]{1,0:T(8,128)} %bitcast.8), custom_call_target="tpu_custom_call" | custom-call | tf_op jit(solution)/shard_map/pallas_call | solution.py:410
  37.0 0.6 %shard_map.104 = (f32[16,128]{1,0:T(8,128)}, f32[3,2048]{1,0:T(4,128)}, f32[1]{0:T(128)}) custom-call(f32[4,16,128]{2,1,0:T(8,128)S(1)} %get-tuple-element.8.slots_in, f32[1,128]{1,0:T(1,128)S(1)} %get-tuple-element.9.least_in), custom_call_target="tpu_custom_call" | custom-call | tf_op jit(solution)/shard_map/pallas_call | solution.py:448

commit v4 on v2

--- a/solution.py
+++ b/solution.py
@@ -48,17 +48,23 @@
     g = lax.axis_index("grp")
     n_dom = lax.axis_size("dom")
     z, y, c = a // 16, (a // 2) % 8, a % 2
-    root = z < 2
+    column = (y == 0) & (c == 0) & (g == 0)
+    zeroth = column & (z == 0)
+    stand_in = (a == 1) & (g == 0)
+    root = (z < 2) & jnp.logical_not(zeroth)
+    children = jnp.where(column, NZ - 1, 7)
     low, high = a > 0, a < n_dom - 1
 
     def dom_of(zz, yy, cc):
         return (zz * NY + yy) * 2 + cc
 
     others = [lax.rem(g + d, NG) for d in (2, 1, 3)]
-    plane = [
-        at(dom_of(z, lax.rem(y + dy, NY), lax.rem(c + dc, 2)), lax.rem(g + dx, NG))
-        for dy in (4, 3, 5, 2, 6, 1, 7, 0) for dx in (2, 1, 3, 0) for dc in (0, 1) if dy or dx or dc
-    ]
+    moves = [(dy, dx, dc) for dy in (4, 3, 5, 2, 6, 1, 7, 0) for dx in (2, 1, 3, 0) for dc in (0, 1) if dy or dx or dc]
+
+    def with_plane(do):
+        for k, (dy, dx, dc) in enumerate(moves):
+            dom, grp = dom_of(z, lax.rem(y + dy, NY), lax.rem(c + dc, 2)), lax.rem(g + dx, NG)
+            pl.when((dom > 0) | (grp > 0))(functools.partial(do, k, at(dom, grp)))
 
     loads = [
         pltpu.make_async_copy(src, dst, load.at[k])
@@ -89,13 +95,19 @@
     @pl.when(root)
     def _():
         def child(k, _):
-            greet(at(dom_of(k, y, c), g))
+            greet(at(dom_of(lax.rem(z + 1 + k, NZ), y, c), g))
             return 0
 
-        lax.fori_loop(2, NZ, child, 0)
-        greet(at(dom_of(1 - z, y, c), g))
-        for p in plane:
-            greet(p)
+        lax.fori_loop(0, NZ - 1, child, 0)
+        with_plane(lambda k, p: greet(p))
+
+    @pl.when(stand_in)
+    def _():
+        def child(k, _):
+            greet(at(dom_of(k, 0, 0), 0))
+            return 0
+
+        lax.fori_loop(0, NZ, child, 0)
 
     lane = lax.broadcasted_iota(jnp.int32, (NB, W), 1)
     sub = lax.broadcasted_iota(jnp.int32, (NB, W), 0)
@@ -110,13 +122,26 @@
     steps = jnp.where(active, CFL * h / jnp.sqrt(GAMMA * (GAMMA - 1.0) * u), 1e30)
     mine[...] = jnp.min(steps, axis=0, keepdims=True)
 
-    wait_for = 3 + jnp.where(low, 1, 0) + jnp.where(high, 1, 0) + jnp.where(root, len(plane) + 1, 2)
+    wait_for = 3 + jnp.where(low, 1, 0) + jnp.where(high, 1, 0) + jnp.where(root, jnp.where(z == 0, len(moves), len(moves) + 1), 2)
     pl.semaphore_wait(barrier, wait_for)
 
-    for zr in range(2):
-        @pl.when(z != zr)
-        def _():
-            remote(mine, zbuf.at[pl.ds(z, 1)], msend.at[zr], mrecv.at[0], at(dom_of(zr, y, c), g)).start()
+    def report(zr):
+        to, row = dom_of(zr, y, c), z
+        if zr == 0:
+            to, row = jnp.where(column, 1, to), jnp.where(column, NZ + z, z)
+        return remote(mine, zbuf.at[pl.ds(row, 1)], msend.at[zr], mrecv.at[0], at(to, g))
+
+    reports = ((0, (z > 0) | zeroth), (1, z != 1))
+    for zr, there in reports:
+        pl.when(there)(lambda zr=zr: report(zr).start())
+
+    @pl.when(root & jnp.logical_not(stand_in))
+    def _():
+        zbuf[NZ : 2 * NZ, :] = jnp.full((NZ, W), 1e30, jnp.float32)
+
+    @pl.when(root & (z == 0))
+    def _():
+        xbuf[0:1, :] = jnp.full((1, W), 1e30, jnp.float32)
 
     for copy in loads[3:]:
         copy.wait()
@@ -284,7 +309,12 @@
 
     def pairs(block):
         coll[...] = jnp.zeros((W, W), jnp.float32)
-        lax.fori_loop(0, NB, block, 0)
+        def two(b, _):
+            block(2 * b, 0)
+            block(2 * b + 1, 0)
+            return 0
+
+        lax.fori_loop(0, NB // 2, two, 0)
         return jnp.transpose(coll[...])
 
     inv_h = 1.0 / h
@@ -345,28 +375,42 @@
     @pl.when(root)
     def _():
         zbuf[pl.ds(z, 1), :] = mine[...]
-        landed(zbuf.at[pl.ds(0, NZ - 1)], mrecv.at[0])
+
+        @pl.when(stand_in)
+        def _():
+            landed(zbuf.at[pl.ds(0, 2 * NZ - 1)], mrecv.at[0])
+
+        @pl.when(jnp.logical_not(stand_in))
+        def _():
+            landed(zbuf.at[pl.ds(0, NZ - 1)], mrecv.at[0])
+
         least = jnp.min(zbuf[...], axis=0, keepdims=True)
         index = (y * 2 + c) * NG + g
         last[...] = least
         xbuf[pl.ds(index, 1), :] = least
-        for k, p in enumerate(plane):
-            remote(last, xbuf.at[pl.ds(index, 1)], msend.at[2 + k], mrecv.at[1], p).start()
+        with_plane(lambda k, p: remote(last, xbuf.at[pl.ds(index, 1)], msend.at[2 + k], mrecv.at[1], p).start())
 
     landed(outbuf.at[pl.ds(0, 3)], orecv)
     slots_out[...] = outbuf[...]
 
     @pl.when(root)
     def _():
-        landed(xbuf.at[pl.ds(0, len(plane))], mrecv.at[1])
+        @pl.when(z == 0)
+        def _():
+            landed(xbuf.at[pl.ds(0, len(moves) - 1)], mrecv.at[1])
+
+        @pl.when(z != 0)
+        def _():
+            landed(xbuf.at[pl.ds(0, len(moves))], mrecv.at[1])
+
         final[...] = jnp.min(xbuf[...], axis=0, keepdims=True)
 
         def child(k, _):
-            to = jnp.where(z == 0, NZ - 1 - k, 2 + k)
-            remote(final, final, msend.at[2 + len(plane) + k], mrecv.at[2], at(dom_of(to, y, c), g)).start()
+            to = jnp.where(z == 0, NZ - 1 - k, lax.rem(2 + k, NZ))
+            remote(final, final, msend.at[65 + k], mrecv.at[2], at(dom_of(to, y, c), g)).start()
             return 0
 
-        lax.fori_loop(0, 7, child, 0)
+        lax.fori_loop(0, children, child, 0)
 
     @pl.when(jnp.logical_not(root))
     def _():
@@ -379,15 +423,18 @@
     on_sides(sent_factors)
     for copy in results:
         copy.wait_send()
-    for zr in range(2):
-        @pl.when(z != zr)
-        def _():
-            landed(mine, msend.at[zr])
+    for zr, there in reports:
+        pl.when(there)(lambda zr=zr: report(zr).wait_send())
 
     @pl.when(root)
     def _():
-        for k in range(len(plane) + 7):
-            landed(last, msend.at[2 + k])
+        with_plane(lambda k, p: landed(last, msend.at[2 + k]))
+
+        def child(k, _):
+            landed(last, msend.at[65 + k])
+            return 0
+
+        lax.fori_loop(0, children, child, 0)
 
 
 def unpack(slots_in, least_in, dens_out, acc_out, ts_out):
@@ -432,12 +479,12 @@
             pltpu.VMEM((NG, 4 * CAP, W), f32),
             pltpu.VMEM((NG, 4 * CAP, W), f32),
             pltpu.VMEM((1, W), f32),
-            pltpu.VMEM((NZ, W), f32),
+            pltpu.VMEM((2 * NZ, W), f32),
             pltpu.VMEM((2 * NY * NG, W), f32),
             pltpu.VMEM((1, W), f32),
             pltpu.VMEM((1, W), f32),
             sem((8,)), sem((3 * NG,)), sem((6,)), sem((3 * NG,)), sem((6,)), sem((3 * NG,)), sem((3,)),
-            sem((3,)), sem, sem((2 + 63 + 7,)), sem((3,)),
+            sem((3,)), sem, sem((2 + 63 + 15,)), sem((3,)),
         ],
         compiler_params=pltpu.CompilerParams(collective_id=0, has_side_effects=True),
     )(

time: 43.8 us -> 36.2 us (0.83)
  Pallas kernels: 42.9 us -> 35.3 us
    pallas_call x1, Pallas kernels: 42.3 us -> 34.7 us  [body(): pl.pallas_call(kernel, out_shape=(pltpu.VMEM((NG, 4 * CAP, W), f32), pltp...]
where the time goes in v4:
time: 36.2 us; the launch traced here: 36 us
  Pallas kernels  35.3 us (98%)
  between operations  0.64 us (2%)
    pallas_call x1, Pallas kernels, body(): pl.pallas_call(kernel, out_shape=(pltpu.VMEM((NG, 4 * CAP, W), f32), pltp...  34.7 us

profile of v4, /device:TPU:1, one launch (start us, length us, event | category | flops | bytes accessed | tf_op | source)
XLA Modules:
  0.0 36.0 jit_solution(1410814467947840555)
XLA Ops:
  0.6 34.7 %shard_map.103 = (f32[4,16,128]{2,1,0:T(8,128)S(1)}, f32[1,128]{1,0:T(1,128)S(1)}) custom-call(s32[8]{0:T(128)} %bitcast.10, s32[4,8]{1,0:T(4,128)} %bitcast.9, s32[8]{0:T(128)} %cnt_in.1, f32[3,1024]{1,0:T(4,128)} %pos_in.1, f32[3,1024]{1,0:T(4,128)} %vel_in.1, f32[8,128]{1,0:T(8,128)} %bitcast.6, f32[8,128]{1,0:T(8,128)} %bitcast.7, f32[8,128]{1,0:T(8,128)} %bitcast.8), custom_call_target="tpu_custom_call" | custom-call | tf_op jit(solution)/shard_map/pallas_call | solution.py:456
  35.3 0.6 %shard_map.104 = (f32[16,128]{1,0:T(8,128)}, f32[3,2048]{1,0:T(4,128)}, f32[1]{0:T(128)}) custom-call(f32[4,16,128]{2,1,0:T(8,128)S(1)} %get-tuple-element.8.slots_in, f32[1,128]{1,0:T(1,128)S(1)} %get-tuple-element.9.least_in), custom_call_target="tpu_custom_call" | custom-call | tf_op jit(solution)/shard_map/pallas_call | solution.py:494

commit v5 on v4

--- a/solution.py
+++ b/solution.py
@@ -52,7 +52,7 @@
     zeroth = column & (z == 0)
     stand_in = (a == 1) & (g == 0)
     root = (z < 2) & jnp.logical_not(zeroth)
-    children = jnp.where(column, NZ - 1, 7)
+    hands_on = z == 4
     low, high = a > 0, a < n_dom - 1
 
     def dom_of(zz, yy, cc):
@@ -191,12 +191,12 @@
 
     def over_group(ref, per, send, recv, d):
         part = piece_at(ref, per, 1, 0)
-        return remote(part, part, send.at[d], recv.at[NG - d], at(a, lax.rem(g + d, NG)))
+        return remote(part, part, send.at[0], recv.at[NG - d - 1], at(a, lax.rem(g + d, NG)))
 
     def to_side(ref, per, send, recv, d, up):
         src, dst = piece_at(ref, per, 1, d), piece_at(ref, per, 0 if up else 2, d)
-        k = NG if up else NG + 1
-        return remote(src, dst, send.at[(k - 3) * NG + d], recv.at[k], at(a + (1 if up else -1), g))
+        k = 1 if up else 2
+        return remote(src, dst, send.at[k], recv.at[k + 2], at(a + (1 if up else -1), g))
 
     def sides(parts, d, do):
         for up, there in ((True, high), (False, low)):
@@ -213,20 +213,21 @@
         between()
         for d in (1, 3, 2):
             for ref, per, send, recv in parts:
-                landed(ref.at[pl.ds(0, per)], recv.at[d])
+                landed(ref.at[pl.ds(0, per)], recv.at[d - 1])
             sides(parts, d, lambda copy: copy.start())
-        for k, there in ((NG, low), (NG + 1, high)):
+        for k, there in ((3, low), (4, high)):
             @pl.when(there)
             def _():
                 for ref, per, send, recv in parts:
                     landed(ref.at[pl.ds(0, NG * per)], recv.at[k])
 
     def sent(parts):
-        for d in (2, 1, 3):
-            for part in parts:
-                over_group(*part, d).wait_send()
-        for d in range(NG):
-            sides(parts, d, lambda copy: copy.wait_send())
+        for k, pieces, there in ((0, 3, None), (1, NG, high), (2, NG, low)):
+            def left():
+                for ref, per, send, recv in parts:
+                    landed(ref.at[pl.ds(0, pieces * per)], send.at[k])
+
+            left() if there is None else pl.when(there)(left)
 
     first = ((pool, 4 * NB, dsend, drecv), (table, 1, tsend, trecv))
 
@@ -310,11 +311,11 @@
     def pairs(block):
         coll[...] = jnp.zeros((W, W), jnp.float32)
         def two(b, _):
-            block(2 * b, 0)
-            block(2 * b + 1, 0)
+            for k in range(4):
+                block(4 * b + k, 0)
             return 0
 
-        lax.fori_loop(0, NB // 2, two, 0)
+        lax.fori_loop(0, NB // 4, two, 0)
         return jnp.transpose(coll[...])
 
     inv_h = 1.0 / h
@@ -335,7 +336,7 @@
         dst = mfpool.at[pl.ds(pl.multiple_of(((1 - i) * NG + g) * NB, NB), NB)]
         to = others if i == 0 else others + [g]
         return [
-            remote(part, dst, fsend.at[(i + 1) * NG + k], frecv.at[1 - i], at(a + i, o)) for k, o in enumerate(to)
+            remote(part, dst, fsend.at[i + 1], frecv.at[1 - i], at(a + i, o)) for k, o in enumerate(to)
         ]
 
     def on_sides(do):
@@ -347,8 +348,7 @@
             copy.start()
 
     def sent_factors(i):
-        for copy in factors(i):
-            copy.wait_send()
+        landed(mfpool.at[pl.ds(0, (3 if i == 0 else NG) * NB)], fsend.at[i + 1])
 
     on_sides(start_factors)
     start_factors(0)
@@ -360,6 +360,24 @@
         here = slice((1 + comp) * NB, (2 + comp) * NB)
         total = 6.0 * ih9 * (res[here, :] + found[comp * NB : (comp + 1) * NB, :])
         res[here, :] = jnp.where(active, total, 0.0)
+
+    @pl.when(root)
+    def _():
+        zbuf[pl.ds(z, 1), :] = mine[...]
+
+        @pl.when(stand_in)
+        def _():
+            landed(zbuf.at[pl.ds(0, 2 * NZ - 1)], mrecv.at[0])
+
+        @pl.when(jnp.logical_not(stand_in))
+        def _():
+            landed(zbuf.at[pl.ds(0, NZ - 1)], mrecv.at[0])
+
+        least = jnp.min(zbuf[...], axis=0, keepdims=True)
+        index = (y * 2 + c) * NG + g
+        last[...] = least
+        xbuf[pl.ds(index, 1), :] = least
+        with_plane(lambda k, p: remote(last, xbuf.at[pl.ds(index, 1)], msend.at[2], mrecv.at[1], p).start())
 
     for t in range(NG):
         for r in range(CAP):
@@ -367,29 +385,11 @@
             for comp in range(4):
                 source = jnp.where(e < NB, comp * NB + e, 4 * NB)
                 outsend[t, comp * CAP + r : comp * CAP + r + 1, :] = res[pl.ds(source, 1), :]
-    results = [remote(outsend.at[o], outbuf.at[g], osend.at[k], orecv, at(a, o)) for k, o in enumerate(others)]
+    results = [remote(outsend.at[o], outbuf.at[g], osend, orecv, at(a, o)) for o in others]
     for copy in results:
         copy.start()
     outbuf[g] = outsend[g]
 
-    @pl.when(root)
-    def _():
-        zbuf[pl.ds(z, 1), :] = mine[...]
-
-        @pl.when(stand_in)
-        def _():
-            landed(zbuf.at[pl.ds(0, 2 * NZ - 1)], mrecv.at[0])
-
-        @pl.when(jnp.logical_not(stand_in))
-        def _():
-            landed(zbuf.at[pl.ds(0, NZ - 1)], mrecv.at[0])
-
-        least = jnp.min(zbuf[...], axis=0, keepdims=True)
-        index = (y * 2 + c) * NG + g
-        last[...] = least
-        xbuf[pl.ds(index, 1), :] = least
-        with_plane(lambda k, p: remote(last, xbuf.at[pl.ds(index, 1)], msend.at[2 + k], mrecv.at[1], p).start())
-
     landed(outbuf.at[pl.ds(0, 3)], orecv)
     slots_out[...] = outbuf[...]
 
@@ -405,36 +405,51 @@
 
         final[...] = jnp.min(xbuf[...], axis=0, keepdims=True)
 
-        def child(k, _):
-            to = jnp.where(z == 0, NZ - 1 - k, lax.rem(2 + k, NZ))
-            remote(final, final, msend.at[65 + k], mrecv.at[2], at(dom_of(to, y, c), g)).start()
-            return 0
-
-        lax.fori_loop(0, children, child, 0)
+    def give(k, to):
+        return remote(final, final, msend.at[k], mrecv.at[2], at(dom_of(to, y, c), g))
+
+    @pl.when(z == 1)
+    def _():
+        for to in (4, 3, 2):
+            give(3, to).start()
+        pl.when(column)(lambda: give(4, 0).start())
 
     @pl.when(jnp.logical_not(root))
     def _():
         landed(final, mrecv.at[2])
+
+    @pl.when(hands_on)
+    def _():
+        for to in range(NZ - 1, 4, -1):
+            give(3, to).start()
 
     least_out[...] = final[...]
 
     sent(first)
     sent_factors(0)
     on_sides(sent_factors)
-    for copy in results:
-        copy.wait_send()
+    landed(outbuf.at[pl.ds(0, 3)], osend)
     for zr, there in reports:
         pl.when(there)(lambda zr=zr: report(zr).wait_send())
 
     @pl.when(root)
     def _():
-        with_plane(lambda k, p: landed(last, msend.at[2 + k]))
-
-        def child(k, _):
-            landed(last, msend.at[65 + k])
-            return 0
-
-        lax.fori_loop(0, children, child, 0)
+        @pl.when(z == 0)
+        def _():
+            landed(xbuf.at[pl.ds(0, len(moves) - 1)], msend.at[2])
+
+        @pl.when(z != 0)
+        def _():
+            landed(xbuf.at[pl.ds(0, len(moves))], msend.at[2])
+
+    @pl.when(z == 1)
+    def _():
+        landed(xbuf.at[pl.ds(0, 3)], msend.at[3])
+        pl.when(column)(lambda: landed(final, msend.at[4]))
+
+    @pl.when(hands_on)
+    def _():
+        landed(xbuf.at[pl.ds(0, NZ - 5)], msend.at[3])
 
 
 def unpack(slots_in, least_in, dens_out, acc_out, ts_out):
@@ -483,8 +498,8 @@
             pltpu.VMEM((2 * NY * NG, W), f32),
             pltpu.VMEM((1, W), f32),
             pltpu.VMEM((1, W), f32),
-            sem((8,)), sem((3 * NG,)), sem((6,)), sem((3 * NG,)), sem((6,)), sem((3 * NG,)), sem((3,)),
-            sem((3,)), sem, sem((2 + 63 + 15,)), sem((3,)),
+            sem((8,)), sem((3,)), sem((5,)), sem((3,)), sem((5,)), sem((3,)), sem((3,)),
+            sem, sem, sem((5,)), sem((3,)),
         ],
         compiler_params=pltpu.CompilerParams(collective_id=0, has_side_effects=True),
     )(

time: 36.2 us -> 34 us (0.939)
  Pallas kernels: 35.3 us -> 33.2 us
    pallas_call x1, Pallas kernels: 34.7 us -> 32.5 us  [body(): pl.pallas_call(kernel, out_shape=(pltpu.VMEM((NG, 4 * CAP, W), f32), pltp...]
where the time goes in v5:
time: 34 us; the launch traced here: 33.8 us
  Pallas kernels  33.2 us (98%)
  between operations  0.64 us (2%)
    pallas_call x1, Pallas kernels, body(): pl.pallas_call(kernel, out_shape=(pltpu.VMEM((NG, 4 * CAP, W), f32), pltp...  32.5 us

profile of v5, /device:TPU:1, one launch (start us, length us, event | category | flops | bytes accessed | tf_op | source)
XLA Modules:
  0.0 33.8 jit_solution(5421353643123862603)
XLA Ops:
  0.6 32.5 %shard_map.103 = (f32[4,16,128]{2,1,0:T(8,128)S(1)}, f32[1,128]{1,0:T(1,128)S(1)}) custom-call(s32[8]{0:T(128)} %bitcast.10, s32[4,8]{1,0:T(4,128)} %bitcast.9, s32[8]{0:T(128)} %cnt_in.1, f32[3,1024]{1,0:T(4,128)} %pos_in.1, f32[3,1024]{1,0:T(4,128)} %vel_in.1, f32[8,128]{1,0:T(8,128)} %bitcast.6, f32[8,128]{1,0:T(8,128)} %bitcast.7, f32[8,128]{1,0:T(8,128)} %bitcast.8), custom_call_target="tpu_custom_call" | custom-call | tf_op jit(solution)/shard_map/pallas_call | solution.py:471
  33.2 0.6 %shard_map.104 = (f32[16,128]{1,0:T(8,128)}, f32[3,2048]{1,0:T(4,128)}, f32[1]{0:T(128)}) custom-call(f32[4,16,128]{2,1,0:T(8,128)S(1)} %get-tuple-element.8.slots_in, f32[1,128]{1,0:T(1,128)S(1)} %get-tuple-element.9.least_in), custom_call_target="tpu_custom_call" | custom-call | tf_op jit(solution)/shard_map/pallas_call | solution.py:509

commit v6 on v5

--- a/solution.py
+++ b/solution.py
@@ -393,38 +393,6 @@
     landed(outbuf.at[pl.ds(0, 3)], orecv)
     slots_out[...] = outbuf[...]
 
-    @pl.when(root)
-    def _():
-        @pl.when(z == 0)
-        def _():
-            landed(xbuf.at[pl.ds(0, len(moves) - 1)], mrecv.at[1])
-
-        @pl.when(z != 0)
-        def _():
-            landed(xbuf.at[pl.ds(0, len(moves))], mrecv.at[1])
-
-        final[...] = jnp.min(xbuf[...], axis=0, keepdims=True)
-
-    def give(k, to):
-        return remote(final, final, msend.at[k], mrecv.at[2], at(dom_of(to, y, c), g))
-
-    @pl.when(z == 1)
-    def _():
-        for to in (4, 3, 2):
-            give(3, to).start()
-        pl.when(column)(lambda: give(4, 0).start())
-
-    @pl.when(jnp.logical_not(root))
-    def _():
-        landed(final, mrecv.at[2])
-
-    @pl.when(hands_on)
-    def _():
-        for to in range(NZ - 1, 4, -1):
-            give(3, to).start()
-
-    least_out[...] = final[...]
-
     sent(first)
     sent_factors(0)
     on_sides(sent_factors)
@@ -441,6 +409,38 @@
         @pl.when(z != 0)
         def _():
             landed(xbuf.at[pl.ds(0, len(moves))], msend.at[2])
+
+    @pl.when(root)
+    def _():
+        @pl.when(z == 0)
+        def _():
+            landed(xbuf.at[pl.ds(0, len(moves) - 1)], mrecv.at[1])
+
+        @pl.when(z != 0)
+        def _():
+            landed(xbuf.at[pl.ds(0, len(moves))], mrecv.at[1])
+
+        final[...] = jnp.min(xbuf[...], axis=0, keepdims=True)
+
+    def give(k, to):
+        return remote(final, final, msend.at[k], mrecv.at[2], at(dom_of(to, y, c), g))
+
+    @pl.when(z == 1)
+    def _():
+        for to in (4, 3, 2):
+            give(3, to).start()
+        pl.when(column)(lambda: give(4, 0).start())
+
+    @pl.when(jnp.logical_not(root))
+    def _():
+        landed(final, mrecv.at[2])
+
+    @pl.when(hands_on)
+    def _():
+        for to in range(NZ - 1, 4, -1):
+            give(3, to).start()
+
+    least_out[...] = final[...]
 
     @pl.when(z == 1)
     def _():

time: 34 us -> 33.9 us (level)
  no operation moved by 1% of the time
where the time goes in v6:
time: 33.9 us; the launch traced here: 33.7 us
  Pallas kernels  33.1 us (98%)
  between operations  0.64 us (2%)
    pallas_call x1, Pallas kernels, body(): pl.pallas_call(kernel, out_shape=(pltpu.VMEM((NG, 4 * CAP, W), f32), pltp...  32.4 us

profile of v6, /device:TPU:1, one launch (start us, length us, event | category | flops | bytes accessed | tf_op | source)
XLA Modules:
  0.0 33.7 jit_solution(3998593348117925134)
XLA Ops:
  0.6 32.4 %shard_map.103 = (f32[4,16,128]{2,1,0:T(8,128)S(1)}, f32[1,128]{1,0:T(1,128)S(1)}) custom-call(s32[8]{0:T(128)} %bitcast.10, s32[4,8]{1,0:T(4,128)} %bitcast.9, s32[8]{0:T(128)} %cnt_in.1, f32[3,1024]{1,0:T(4,128)} %pos_in.1, f32[3,1024]{1,0:T(4,128)} %vel_in.1, f32[8,128]{1,0:T(8,128)} %bitcast.6, f32[8,128]{1,0:T(8,128)} %bitcast.7, f32[8,128]{1,0:T(8,128)} %bitcast.8), custom_call_target="tpu_custom_call" | custom-call | tf_op jit(solution)/shard_map/pallas_call | solution.py:471
  33.1 0.6 %shard_map.104 = (f32[16,128]{1,0:T(8,128)}, f32[3,2048]{1,0:T(4,128)}, f32[1]{0:T(128)}) custom-call(f32[4,16,128]{2,1,0:T(8,128)S(1)} %get-tuple-element.8.slots_in, f32[1,128]{1,0:T(1,128)S(1)} %get-tuple-element.9.least_in), custom_call_target="tpu_custom_call" | custom-call | tf_op jit(solution)/shard_map/pallas_call | solution.py:509

commit v7 on v6

--- a/solution.py
+++ b/solution.py
@@ -42,7 +42,7 @@
     tgt, nbr, cnt, pos, vel, smooth, mass, energy, base_of,
     pool, mfpool, table, rows, cols, stash, coll, res, outsend, outbuf,
     mine, zbuf, xbuf, last, final,
-    load, dsend, drecv, tsend, trecv, fsend, frecv, osend, orecv, msend, mrecv,
+    load, drecv, trecv, frecv, orecv, mrecv,
 ):
     a = lax.axis_index("dom")
     g = lax.axis_index("grp")
@@ -129,7 +129,7 @@
         to, row = dom_of(zr, y, c), z
         if zr == 0:
             to, row = jnp.where(column, 1, to), jnp.where(column, NZ + z, z)
-        return remote(mine, zbuf.at[pl.ds(row, 1)], msend.at[zr], mrecv.at[0], at(to, g))
+        return remote(mine, zbuf.at[pl.ds(row, 1)], load.at[zr], mrecv.at[0], at(to, g))
 
     reports = ((0, (z > 0) | zeroth), (1, z != 1))
     for zr, there in reports:
@@ -191,12 +191,12 @@
 
     def over_group(ref, per, send, recv, d):
         part = piece_at(ref, per, 1, 0)
-        return remote(part, part, send.at[0], recv.at[NG - d - 1], at(a, lax.rem(g + d, NG)))
+        return remote(part, part, load.at[send[0]], recv.at[NG - d - 1], at(a, lax.rem(g + d, NG)))
 
     def to_side(ref, per, send, recv, d, up):
         src, dst = piece_at(ref, per, 1, d), piece_at(ref, per, 0 if up else 2, d)
         k = 1 if up else 2
-        return remote(src, dst, send.at[k], recv.at[k + 2], at(a + (1 if up else -1), g))
+        return remote(src, dst, load.at[send[k]], recv.at[k + 2], at(a + (1 if up else -1), g))
 
     def sides(parts, d, do):
         for up, there in ((True, high), (False, low)):
@@ -225,11 +225,11 @@
         for k, pieces, there in ((0, 3, None), (1, NG, high), (2, NG, low)):
             def left():
                 for ref, per, send, recv in parts:
-                    landed(ref.at[pl.ds(0, pieces * per)], send.at[k])
+                    landed(ref.at[pl.ds(0, pieces * per)], load.at[send[k]])
 
             left() if there is None else pl.when(there)(left)
 
-    first = ((pool, 4 * NB, dsend, drecv), (table, 1, tsend, trecv))
+    first = ((pool, 4 * NB, (3, 4, 5), drecv), (table, 1, (6, 7, 2), trecv))
 
     def columns():
         rows[3 * NB : 4 * NB, :] = h * h
@@ -336,7 +336,7 @@
         dst = mfpool.at[pl.ds(pl.multiple_of(((1 - i) * NG + g) * NB, NB), NB)]
         to = others if i == 0 else others + [g]
         return [
-            remote(part, dst, fsend.at[i + 1], frecv.at[1 - i], at(a + i, o)) for k, o in enumerate(to)
+            remote(part, dst, load.at[i + 4], frecv.at[1 - i], at(a + i, o)) for k, o in enumerate(to)
         ]
 
     def on_sides(do):
@@ -348,8 +348,9 @@
             copy.start()
 
     def sent_factors(i):
-        landed(mfpool.at[pl.ds(0, (3 if i == 0 else NG) * NB)], fsend.at[i + 1])
-
+        landed(mfpool.at[pl.ds(0, (3 if i == 0 else NG) * NB)], load.at[i + 4])
+
+    sent(first)
     on_sides(start_factors)
     start_factors(0)
     landed(mfpool.at[pl.ds(0, 3 * NB)], frecv.at[1])
@@ -377,7 +378,7 @@
         index = (y * 2 + c) * NG + g
         last[...] = least
         xbuf[pl.ds(index, 1), :] = least
-        with_plane(lambda k, p: remote(last, xbuf.at[pl.ds(index, 1)], msend.at[2], mrecv.at[1], p).start())
+        with_plane(lambda k, p: remote(last, xbuf.at[pl.ds(index, 1)], load.at[7], mrecv.at[1], p).start())
 
     for t in range(NG):
         for r in range(CAP):
@@ -385,7 +386,7 @@
             for comp in range(4):
                 source = jnp.where(e < NB, comp * NB + e, 4 * NB)
                 outsend[t, comp * CAP + r : comp * CAP + r + 1, :] = res[pl.ds(source, 1), :]
-    results = [remote(outsend.at[o], outbuf.at[g], osend, orecv, at(a, o)) for o in others]
+    results = [remote(outsend.at[o], outbuf.at[g], load.at[6], orecv, at(a, o)) for o in others]
     for copy in results:
         copy.start()
     outbuf[g] = outsend[g]
@@ -393,10 +394,9 @@
     landed(outbuf.at[pl.ds(0, 3)], orecv)
     slots_out[...] = outbuf[...]
 
-    sent(first)
     sent_factors(0)
     on_sides(sent_factors)
-    landed(outbuf.at[pl.ds(0, 3)], osend)
+    landed(outbuf.at[pl.ds(0, 3)], load.at[6])
     for zr, there in reports:
         pl.when(there)(lambda zr=zr: report(zr).wait_send())
 
@@ -404,11 +404,11 @@
     def _():
         @pl.when(z == 0)
         def _():
-            landed(xbuf.at[pl.ds(0, len(moves) - 1)], msend.at[2])
+            landed(xbuf.at[pl.ds(0, len(moves) - 1)], load.at[7])
 
         @pl.when(z != 0)
         def _():
-            landed(xbuf.at[pl.ds(0, len(moves))], msend.at[2])
+            landed(xbuf.at[pl.ds(0, len(moves))], load.at[7])
 
     @pl.when(root)
     def _():
@@ -423,13 +423,13 @@
         final[...] = jnp.min(xbuf[...], axis=0, keepdims=True)
 
     def give(k, to):
-        return remote(final, final, msend.at[k], mrecv.at[2], at(dom_of(to, y, c), g))
+        return remote(final, final, load.at[k], mrecv.at[2], at(dom_of(to, y, c), g))
 
     @pl.when(z == 1)
     def _():
         for to in (4, 3, 2):
-            give(3, to).start()
-        pl.when(column)(lambda: give(4, 0).start())
+            give(2, to).start()
+        pl.when(column)(lambda: give(7, 0).start())
 
     @pl.when(jnp.logical_not(root))
     def _():
@@ -438,18 +438,18 @@
     @pl.when(hands_on)
     def _():
         for to in range(NZ - 1, 4, -1):
-            give(3, to).start()
+            give(2, to).start()
 
     least_out[...] = final[...]
 
     @pl.when(z == 1)
     def _():
-        landed(xbuf.at[pl.ds(0, 3)], msend.at[3])
-        pl.when(column)(lambda: landed(final, msend.at[4]))
+        landed(xbuf.at[pl.ds(0, 3)], load.at[2])
+        pl.when(column)(lambda: landed(final, load.at[7]))
 
     @pl.when(hands_on)
     def _():
-        landed(xbuf.at[pl.ds(0, NZ - 5)], msend.at[3])
+        landed(xbuf.at[pl.ds(0, NZ - 5)], load.at[2])
 
 
 def unpack(slots_in, least_in, dens_out, acc_out, ts_out):
@@ -498,8 +498,7 @@
             pltpu.VMEM((2 * NY * NG, W), f32),
             pltpu.VMEM((1, W), f32),
             pltpu.VMEM((1, W), f32),
-            sem((8,)), sem((3,)), sem((5,)), sem((3,)), sem((5,)), sem((3,)), sem((3,)),
-            sem, sem, sem((5,)), sem((3,)),
+            sem((8,)), sem((5,)), sem((5,)), sem((3,)), sem, sem((3,)),
         ],
         compiler_params=pltpu.CompilerParams(collective_id=0, has_side_effects=True),
     )(

time: 33.9 us -> 33.9 us (level)
  no operation moved by 1% of the time
where the time goes in v7:
time: 33.9 us; the launch traced here: 33.7 us
  Pallas kernels  33 us (97%)
  between operations  0.64 us (2%)
    pallas_call x1, Pallas kernels, body(): pl.pallas_call(kernel, out_shape=(pltpu.VMEM((NG, 4 * CAP, W), f32), pltp...  32.4 us

profile of v7, /device:TPU:1, one launch (start us, length us, event | category | flops | bytes accessed | tf_op | source)
XLA Modules:
  0.0 33.7 jit_solution(9729632860722866920)
XLA Ops:
  0.6 32.4 %shard_map.103 = (f32[4,16,128]{2,1,0:T(8,128)S(1)}, f32[1,128]{1,0:T(1,128)S(1)}) custom-call(s32[8]{0:T(128)} %bitcast.10, s32[4,8]{1,0:T(4,128)} %bitcast.9, s32[8]{0:T(128)} %cnt_in.1, f32[3,1024]{1,0:T(4,128)} %pos_in.1, f32[3,1024]{1,0:T(4,128)} %vel_in.1, f32[8,128]{1,0:T(8,128)} %bitcast.6, f32[8,128]{1,0:T(8,128)} %bitcast.7, f32[8,128]{1,0:T(8,128)} %bitcast.8), custom_call_target="tpu_custom_call" | custom-call | tf_op jit(solution)/shard_map/pallas_call | solution.py:471
  33.0 0.6 %shard_map.104 = (f32[16,128]{1,0:T(8,128)}, f32[3,2048]{1,0:T(4,128)}, f32[1]{0:T(128)}) custom-call(f32[4,16,128]{2,1,0:T(8,128)S(1)} %get-tuple-element.8.slots_in, f32[1,128]{1,0:T(1,128)S(1)} %get-tuple-element.9.least_in), custom_call_target="tpu_custom_call" | custom-call | tf_op jit(solution)/shard_map/pallas_call | solution.py:508
